TPU v7x, 32 devices: a whole 2x2x4 slice. The times are simulated.
32 devices in a mesh: gx: 4 (over z), gy: 2 (over x), gz: 4 (over y, core).
Axes of the slice: x: 2, y: 2, z: 4, core: 2. Of those that a mesh axis runs over, the one named last changes fastest.
Arguments:
- old_slots: bfloat16 [4, 2, 32, 4096], P('gx', 'gy', 'gz'), may hold values from -6 to 6
- old_ids: int32 [4, 2, 32], P('gx', 'gy', 'gz'), may hold values from -1 to 31, as said below
- old_owner: int32 [4, 2, 32], P('gx', 'gy'), may hold values from 0 to 3, as said below
- coefficient: float32 [64, 32, 512], P('gx', 'gy', 'gz'), may hold values from 0.2 to 5
Outputs:
- solution: float32 [64, 32, 512], P('gx', 'gy', 'gz')
Inputs may be any that keep to these rules, and one draw needn't show every extreme that they name: old_owner[a, c, b] is the index along gz of the device that held box b of box column (a, c) before the move; no device holds more than 8 boxes of a column and some device holds exactly 8; no device holds more than 2 of the 8 boxes with one value of b // 8, and that bound is reached. old_ids[a, c, g * 8 + q] is the box held in slot q of device g of box column (a, c), or -1 for an empty slot; it agrees with old_owner and each box stands in exactly one slot.
All inputs are finite; a program needn't handle non-finite values.
Results may differ from a plain program's by a relative error of at most 0.0003.
Values may be sent and summed in bfloat16 or wider, within the bound.
A program may use at most 64 MiB of HBM per device.

v0:
```python
import functools

import jax
import jax.numpy as jnp
from jax import lax
from jax.experimental import pallas as pl
from jax.experimental.pallas import tpu as pltpu
from jax.sharding import PartitionSpec as P

BOX = 16
SEND = 2
W = 4
F32 = jnp.float32
MESH = pl.DeviceIdType.MESH
HIGH = lax.Precision.HIGHEST


def iota(shape, dim):
    return lax.broadcasted_iota(jnp.int32, shape, dim)


def up(v, axis):
    return pltpu.roll(v, 1, axis)


def down(v, axis):
    return pltpu.roll(v, v.shape[axis] - 1, axis)


class Level:
    def __init__(self, x, y, z):
        self.x, self.y, self.z = x, y, z
        self.xe, self.ye = x + 2 * W, y + 2 * W
        self.ze = 128 if z + 2 * W <= 128 else z + 128
        self.shape = (self.xe, self.ye, self.ze)


NEAR = [(a, b, c) for c in (-1, 0, 1) for b in (-1, 0, 1) for a in (-1, 0, 1) if (a, b, c) != (0, 0, 0)]


def near(offset, counts):
    target, exists = {}, None
    for axis, step in zip(("gx", "gy", "gz"), offset):
        me, n = lax.axis_index(axis), counts[axis]
        if step:
            target[axis] = lax.rem(me + step + n, n)
            inside = me > 0 if step < 0 else me < n - 1
            exists = inside if exists is None else jnp.logical_and(exists, inside)
    return target, exists


def exchange(lv, v, bufs, counts):
    py, ly, pz, lz, sends, recvs = bufs
    own = slice(W, W + lv.x)
    py[0] = v[own, 0:W, 0:128]
    py[1] = v[own, lv.y - W : lv.y, 0:128]
    lane = iota((lv.y, 128), 1)
    packed = jnp.zeros((lv.y, 128), F32)
    for k in range(lv.x):
        plane = v[W + k, 0 : lv.y, 0:128]
        if lv.z == 64:
            plane = jnp.where(lane >= 64, pltpu.roll(plane, 64, 1), plane)
        packed = jnp.where(lane // 8 == k, pltpu.roll(plane, (8 * k + W) % 128, 1), packed)
    pz[...] = packed
    block = (pl.ds(0, lv.y), pl.ds(0, 128))
    taken = {-1: (0, W), 0: (0, lv.x), 1: (lv.x - W, W)}
    landed = {-1: lv.x + W, 0: W, 1: 0}
    copies = []
    for at, (a, b, c) in enumerate(NEAR):
        target, exists = near((a, b, c), counts)
        first, count = taken[a]
        if c:
            src, dst = pz, lz.at[(1 - c) // 2, 1 - a, 1 - b]
        elif b:
            side = (b + 1) // 2
            src, dst = py.at[side, pl.ds(first, count)], ly.at[side, pl.ds(landed[a], count)]
        else:
            src, dst = v.at[(pl.ds(W + first, count),) + block], v.at[(pl.ds(landed[a], count),) + block]
        copy = pltpu.make_async_remote_copy(
            src, dst, sends.at[at], recvs.at[at], device_id=target, device_id_type=MESH)
        copies.append(((a, b, c), copy, exists))
    for _, copy, exists in reversed(copies):
        pl.when(exists)(copy.start)
    yield
    for (a, b, c), copy, exists in copies:
        pl.when(exists)(copy.wait_send)
        pl.when(near((-a, -b, -c), counts)[1])(copy.wait_recv)
    v[:, lv.y : lv.y + W, 0:128] = ly[0]
    v[:, lv.y + W : lv.ye, 0:128] = ly[1]
    row = iota((8, 128), 0)
    side = iota((lv.ye, 128), 1)
    edge = (side < W) | (side >= 128 - W)
    for a in range(3):
        parts = []
        for c in range(2):
            ends = jnp.where(row < W, lz[c, a, 2, 0:8, :], lz[c, a, 0, lv.y - 8 : lv.y, :])
            parts.append(jnp.concatenate([lz[c, a, 1], ends], axis=0))
        both = jnp.where(side % 8 >= W, parts[1], parts[0])
        first = (0, W, lv.x + W)[a]
        start, count = ((lv.x - W, W), (0, lv.x), (0, W))[a]
        for k in range(count):
            x = first + k
            strip = jnp.where(edge, pltpu.roll(both, (256 - 8 * (start + k) - W) % 128, 1), 0.0)
            if lv.z == 64:
                v[x] = jnp.where(side < 64, v[x], jnp.where(side >= 128 - W, strip, pltpu.roll(strip, 64, 1)))
            else:
                v[x, :, lv.z : lv.z + 128] = strip
    yield


def gather(buf, sends, recvs, counts):
    me = {axis: lax.axis_index(axis) for axis in counts}
    nx, ny, nz = counts["gx"], counts["gy"], counts["gz"]

    def run(steps, base):
        copies = []
        for at, (target, mine, theirs) in enumerate(steps):
            pair = (sends.at[base + at], recvs.at[base + at])
            copy = pltpu.make_async_remote_copy(mine, mine, *pair, device_id=target, device_id_type=MESH)
            copy.start()
            copies.append((copy, pltpu.make_async_remote_copy(
                theirs, theirs, *pair, device_id=target, device_id_type=MESH)))
        yield
        for copy, arrive in copies:
            copy.wait_send()
            arrive.wait_recv()

    steps = []
    for b in range(ny):
        for c in range(nz):
            if b or c:
                target = {"gy": lax.rem(me["gy"] + b, ny), "gz": lax.rem(me["gz"] + c, nz)}
                source = buf.at[me["gx"], lax.rem(me["gy"] + ny - b, ny), lax.rem(me["gz"] + nz - c, nz)]
                steps.append((target, buf.at[me["gx"], me["gy"], me["gz"]], source))
    yield from run(steps, 0)
    base = len(steps)
    steps = [({"gx": lax.rem(me["gx"] + a, nx)}, buf.at[me["gx"]], buf.at[lax.rem(me["gx"] + nx - a, nx)]) for a in range(1, nx)]
    yield from run(steps, base)


def drain(*steps):
    steps = list(steps)
    while steps:
        steps = [step for step in steps if next(step, steps) is not steps]


def batches(low, high, size, body):
    whole = (high - low) // size
    if whole:
        def run(step, carry):
            body(low + step * size, size)
            return carry

        lax.fori_loop(0, whole, run, 0)
    if low + whole * size < high:
        body(low + whole * size, high - low - whole * size)


def prepare(lv, k, fx, fy, fz, dd, iv):
    def body(first, count):
        made = []
        for x in [first + i for i in range(count)]:
            kx = k[x]
            below = 0.5 * (k[jnp.maximum(x - 1, 0)] + kx)
            above = 0.5 * (kx + k[jnp.minimum(x + 1, lv.xe - 1)])
            second = 0.5 * (up(kx, 0) + kx)
            third = 0.5 * (up(kx, 1) + kx)
            total = below + above + second + down(second, 0) + third + down(third, 1)
            made.append((x, below, second, third, total, jnp.where(kx > 0.0, 1.0 / total, 0.0)))
        for x, *values in made:
            for ref, value in zip((fx, fy, fz, dd, iv), values):
                ref[x] = value

    batches(0, lv.xe, 4 if lv.ze == 128 else 2, body)


def around(v, x, mid, faces):
    fx, fy, fz = faces
    second, third = fy[x], fz[x]
    summed = fx[x] * v[x - 1] + fx[x + 1] * v[x + 1]
    summed = summed + second * up(mid, 0) + down(second * mid, 0)
    return summed + third * up(mid, 1) + down(third * mid, 1)


def half_sweep(lv, v, g, faces, iv, colour, reach):
    parity = iota((lv.ye, lv.ze), 0) + iota((lv.ye, lv.ze), 1)

    def body(first, count):
        fresh = []
        for x in [first + i for i in range(count)]:
            mid = v[x]
            value = (g[x] + around(v, x, mid, faces)) * iv[x]
            fresh.append((x, jnp.where(((parity + x) & 1) == colour, value, mid)))
        for x, value in fresh:
            v[x] = value

    batches(W - reach, W + lv.x + reach, 10 if lv.ze == 128 else 6, body)


def residual_pairs(lv, v, g, faces, dd, pairs):
    def body(first, count):
        made = []
        for i in [first + j for j in range(count)]:
            total = jnp.zeros((lv.ye, lv.ze), F32)
            for k in range(2):
                x = W + 2 * i + k
                mid = v[x]
                total = total + (g[x] - dd[x] * mid + around(v, x, mid, faces))
            made.append((i, total))
        for i, total in made:
            pairs[i] = total[0 : lv.y, 0:128]

    batches(0, lv.x // 2, 4, body)


def open_halo(lv, p, v, g, dd):
    parity = iota((lv.ye, lv.ze), 0) + iota((lv.ye, lv.ze), 1)

    def body(first, count):
        made = []
        for x in [first + i for i in range(count)]:
            red = ((parity + x) & 1) == 0
            px = p[x]
            made.append((x, jnp.where(red, px, 0.0), jnp.where(red, px * dd[x], px)))
        for x, value, source in made:
            v[x] = value
            g[x] = source

    batches(0, lv.xe, 4, body)


def fold_rows(pairs, rows):
    return pairs[:, pl.ds(0, rows, stride=2), :] + pairs[:, pl.ds(1, rows, stride=2), :]


def dot(a, b):
    return jnp.dot(a, b, precision=HIGH, preferred_element_type=F32)


def coarse_mid(pairs, x, y):
    folded = fold_rows(pairs, y // 2).reshape((x // 2) * (y // 2), 128)
    matrix = jnp.where(iota((128, 128), 0) // 2 == iota((128, 128), 1), 0.125, 0.0).astype(F32)
    return dot(folded, matrix).reshape(x // 2, y // 2, 128)


def coarse_low(pairs, count, rows, lanes, tmp, target):
    total = jnp.zeros((rows, 128), F32)
    source, goal = iota((128, 128), 0), iota((128, 128), 1)
    for x in range(count):
        matrix = jnp.where((source // 2 + x * lanes == goal) & (source < 2 * lanes), 0.125, 0.0).astype(F32)
        total = total + dot(pairs[x], matrix)
    tmp[...] = total
    half = rows // 2
    small = tmp[pl.ds(0, half, stride=2), :] + tmp[pl.ds(1, half, stride=2), :]
    target[0:half, :] = small
    target[half:rows, :] = small


def spread_low(buf, whole, counts, pad):
    lane, row = iota((8, 128), 1), iota((8, 128), 0)

    def body(a, carry):
        for i in range(4):
            for ct in range(counts["gy"] // 2):
                for gt in range(counts["gz"] // 4):
                    total = jnp.zeros((8, 128), F32)
                    for c in range(2):
                        for g in range(4):
                            piece = pltpu.roll(buf[a, 2 * ct + c, 4 * gt + g], (32 * (g - i)) % 128, 1)
                            total = jnp.where((lane // 32 == g) & (row // 4 == c), piece, total)
                    whole[pad + 4 * a + i, 8 * ct : 8 * ct + 8, 128 * gt : 128 * gt + 128] = total
        return carry

    lax.fori_loop(0, counts["gx"], body, 0)


def bottom(f, k, s, vv, xs, dims):
    planes, rows, lanes = dims
    row, lane = iota((rows, lanes), 0), iota((rows, lanes), 1)
    edges = (row > 0, row < rows - 1, lane > 0, lane < lanes - 1)

    def shifted(v):
        return (
            jnp.where(edges[0], up(v, 0), 0.0), jnp.where(edges[1], down(v, 0), 0.0),
            jnp.where(edges[2], up(v, 1), 0.0), jnp.where(edges[3], down(v, 1), 0.0))

    def operate(v, x):
        kx, mid = k[x], v[x]
        summed, diagonal = jnp.zeros_like(mid), jnp.zeros_like(mid)
        others = ((k[x - 1], v[x - 1]), (k[x + 1], v[x + 1])) + tuple(zip(shifted(kx), shifted(mid)))
        for other, value in others:
            face = 0.5 * (kx + other)
            diagonal = diagonal + face
            summed = summed + face * value
        return mid, (diagonal * mid - summed) * 0.0625

    zero = jnp.zeros((rows, lanes), F32)

    def first(x, carry):
        mid, image = operate(f, x + 1)
        vv[x] = image
        return carry[0] + mid * mid, carry[1] + mid * image

    def total(v):
        return jnp.sum(jnp.sum(v, axis=0, keepdims=True), axis=1, keepdims=True)

    norm, along = lax.fori_loop(0, planes, first, (zero, zero))
    alpha = total(norm) / total(along)

    def rest(x, carry):
        s[x + 1] = f[x + 1] - alpha * vv[x]
        return carry

    lax.fori_loop(0, planes, rest, 0)

    def second(x, carry):
        mid, image = operate(s, x + 1)
        return carry[0] + image * mid, carry[1] + image * image

    turned, norm = lax.fori_loop(0, planes, second, (zero, zero))
    omega = total(turned) / total(norm)

    def join(x, carry):
        xs[x + 2] = alpha * f[x + 1] + omega * s[x + 1]
        return carry

    lax.fori_loop(0, planes, join, 0)


def pack_boxes(slots, ids, outgoing, boxes, groups):
    held = ids[0].astype(F32)
    cap = held.shape[1]
    eye = iota((cap, cap), 0) == iota((cap, cap), 1)
    rows = jnp.broadcast_to(held, (cap, cap))
    cols = jnp.broadcast_to(jnp.sum(jnp.where(eye, rows, 0.0), axis=1, keepdims=True), (cap, cap))

    def target(v):
        return jnp.floor((v + 0.5) * (1.0 / boxes))

    earlier = (target(rows) == target(cols)) & (cols < rows) & (cols >= 0.0)
    ranking = jnp.sum(jnp.where(earlier, 1.0, 0.0), axis=0, keepdims=True)
    send_row = jnp.where(held >= 0.0, target(held) * SEND + ranking, -1.0)
    count = groups * SEND
    picker = jnp.where(iota((count, cap), 0).astype(F32) == jnp.broadcast_to(send_row, (count, cap)), 1.0, 0.0)
    data = slots[0, 0].astype(F32)
    total = jnp.zeros((count, data.shape[1]), F32)
    for q in range(cap):
        total = total + picker[:, q : q + 1] * data[q : q + 1, :]
    for t in range(groups):
        outgoing[t] = total[SEND * t : SEND * t + SEND, :]


def place_boxes(incoming, owner, lhs, rhs, boxes, groups):
    me = lax.axis_index("gz")
    owners = jnp.broadcast_to(owner[0].astype(F32), (boxes, owner.shape[2]))
    here = iota(owners.shape, 1) == iota(owners.shape, 0) + me * boxes
    col = jnp.sum(jnp.where(here, owners, 0.0), axis=1, keepdims=True)
    cols = jnp.broadcast_to(col, (boxes, boxes))
    first, second = iota((boxes, boxes), 0), iota((boxes, boxes), 1)
    row = jnp.sum(jnp.where(first == second, cols, 0.0), axis=0, keepdims=True)
    before = (jnp.broadcast_to(row, (boxes, boxes)) == cols) & (second < first)
    pick = col * SEND + jnp.sum(jnp.where(before, 1.0, 0.0), axis=1, keepdims=True)
    face = BOX * BOX
    mine = iota((BOX, face), 1) // BOX == iota((BOX, face), 0)
    for i in range(BOX):
        chosen = jnp.zeros((boxes, face), F32)
        for r in range(groups * SEND):
            chosen = jnp.where(pick == float(r), incoming[r // SEND, r % SEND : r % SEND + 1, face * i : face * i + face], chosen)
        for b in range(boxes):
            piece = jnp.where(mine, jnp.broadcast_to(chosen[b : b + 1, :], (BOX, face)), 0.0)
            lhs[BOX * i : BOX * i + BOX, face * b : face * b + face] = piece.astype(jnp.bfloat16)
    return jnp.dot(lhs[...], rhs[...], preferred_element_type=F32)


def kernel(fine, mid, counts, names, slots, ids, owner, coef, out, *scratch):
    r = dict(zip(names, scratch))
    groups = counts["gz"]
    boxes = fine.z // BOX
    at = {axis: lax.axis_index(axis) for axis in counts}
    for name in ("K0", "P0", "Q0", "K1", "P1", "E1", "ly", "lz", "lym", "lzm", "f2", "k2", "s2", "x2"):
        r[name][...] = jnp.zeros(r[name].shape, F32)

    barrier = pltpu.get_barrier_semaphore()
    expected = 0
    for offset in NEAR:
        target, exists = near(offset, counts)

        @pl.when(exists)
        def _():
            pl.semaphore_signal(barrier, inc=1, device_id=target, device_id_type=MESH)

        expected = expected + jnp.where(exists, 1, 0)
    others = [{"gx": lax.rem(at["gx"] + k, counts["gx"])} for k in range(1, counts["gx"])]
    for b in range(counts["gy"]):
        for c in range(groups):
            if b or c:
                others.append({"gy": lax.rem(at["gy"] + b, counts["gy"]), "gz": lax.rem(at["gz"] + c, groups)})
    for target in others:
        pl.semaphore_signal(barrier, inc=1, device_id=target, device_id_type=MESH)

    pack_boxes(slots, ids, r["outgoing"], boxes, groups)
    K0, K1 = r["K0"], r["K1"]
    K0[W : W + fine.x, 0 : fine.y, 0:128] = coef[...]
    for i in range(mid.x):
        r["pairs"][i] = coef[2 * i] + coef[2 * i + 1]
    K1[W : W + mid.x, 0 : mid.y, :] = coarse_mid(r["pairs"], fine.x, fine.y)
    for i in range(mid.x // 2):
        r["pairsm"][i] = K1[W + 2 * i, 0 : mid.y, :] + K1[W + 2 * i + 1, 0 : mid.y, :]
    here = (at["gx"], at["gy"], at["gz"])
    coarse_low(r["pairsm"], mid.x // 2, mid.y, mid.z // 2, r["tmp"], r["gk"].at[here])
    pl.semaphore_wait(barrier, expected + len(others))

    moves = []
    me = at["gz"]
    for k in range(1, groups):
        to, source = lax.rem(me + k, groups), lax.rem(me + groups - k, groups)
        copy = pltpu.make_async_remote_copy(
            r["outgoing"].at[to], r["incoming"].at[me], r["ms"].at[k - 1], r["mr"].at[k - 1],
            device_id={"gz": to}, device_id_type=MESH)
        copy.start()
        arrive = pltpu.make_async_remote_copy(
            r["outgoing"].at[to], r["incoming"].at[source], r["ms"].at[k - 1], r["mr"].at[k - 1],
            device_id={"gz": to}, device_id_type=MESH)
        moves.append((copy, arrive))
    r["incoming"][me] = r["outgoing"][me]

    def bufs(n, tail):
        return tuple(r[b + tail].at[n] for b in ("py", "ly", "pz", "lz", "es", "er"))

    fine_halo, mid_halo = exchange(fine, K0, bufs(0, ""), counts), exchange(mid, K1, bufs(0, "m"), counts)
    low_gather = gather(r["gk"], r["gs"].at[0], r["gr"].at[0], counts)
    for step in (fine_halo, mid_halo, low_gather):
        next(step)
    lane = iota((BOX * BOX, 128), 1)
    folded = iota((BOX * BOX, 128), 0) % BOX == lane % BOX
    for b in range(boxes):
        block = jnp.where(folded & (lane // BOX == b), 1.0, 0.0)
        r["rhs"][BOX * BOX * b : BOX * BOX * (b + 1), :] = block.astype(jnp.bfloat16)
    for copy, arrive in moves:
        copy.wait_send()
        arrive.wait_recv()
    source = place_boxes(r["incoming"], owner, r["lhs"], r["rhs"], boxes, groups)
    source = source.reshape(fine.x, fine.y, 128)
    drain(fine_halo)

    faces0 = (r["fx0"], r["fy0"], r["fz0"])
    faces1 = (r["fx1"], r["fy1"], r["fz1"])
    dd0, iv0, dd1, iv1 = r["dd0"], r["iv0"], r["dd1"], r["iv1"]
    v0, g0, v1, g1 = r["v0"], r["g0"], r["v1"], r["g1"]
    prepare(fine, K0, *faces0, dd0, iv0)
    parity = iota((fine.y, 128), 0) + iota((fine.y, 128), 1)
    for x in range(fine.x):
        red = (parity + x) % 2 == 0
        r["P0"][W + x, 0 : fine.y, 0:128] = jnp.where(red, source[x] * iv0[W + x, 0 : fine.y, 0:128], source[x])
    step = exchange(fine, r["P0"], bufs(1, ""), counts)
    next(step)
    drain(mid_halo)
    prepare(mid, K1, *faces1, dd1, iv1)
    next(low_gather)
    drain(step)
    open_halo(fine, r["P0"], v0, g0, dd0)
    for reach, colour in ((3, 1), (2, 0), (1, 1)):
        half_sweep(fine, v0, g0, faces0, iv0, colour, reach)
    residual_pairs(fine, v0, g0, faces0, dd0, r["pairs"])

    source1 = coarse_mid(r["pairs"], fine.x, fine.y)
    parity = iota((mid.y, 128), 0) + iota((mid.y, 128), 1)
    for x in range(mid.x):
        red = (parity + x) % 2 == 0
        scaled = 4.0 * source1[x]
        r["P1"][W + x, 0 : mid.y, :] = jnp.where(red, scaled * iv1[W + x, 0 : mid.y, :], scaled)
    step = exchange(mid, r["P1"], bufs(1, "m"), counts)
    next(step)
    drain(low_gather)
    spread_low(r["gk"], r["k2"], counts, 1)
    drain(step)
    open_halo(mid, r["P1"], v1, g1, dd1)
    for reach, colour in ((3, 1), (2, 0), (1, 1)):
        half_sweep(mid, v1, g1, faces1, iv1, colour, reach)
    residual_pairs(mid, v1, g1, faces1, dd1, r["pairsm"])
    for i in range(mid.x // 2):
        r["pairsm"][i] = r["pairsm"][i] * 0.25
    coarse_low(r["pairsm"], mid.x // 2, mid.y, mid.z // 2, r["tmp"], r["gf"].at[here])
    r["E1"][W : W + mid.x, 0 : mid.y, :] = v1[W : W + mid.x, 0 : mid.y, :]
    drain(
        gather(r["gf"], r["gs"].at[1], r["gr"].at[1], counts),
        exchange(mid, r["E1"], bufs(2, "m"), counts))

    planes, rows, lanes = 4 * counts["gx"], 4 * counts["gy"], 32 * counts["gz"]
    spread_low(r["gf"], r["f2"], counts, 1)
    bottom(r["f2"], r["k2"], r["s2"], r["v2"], r["x2"], (planes, rows, lanes))
    row8 = iota((8, lanes), 0)
    for q in range(8):
        plane = r["x2"][4 * at["gx"] + q]
        turned = plane
        for c in range(1, counts["gy"]):
            turned = jnp.where(at["gy"] == c, pltpu.roll(plane, rows - 4 * c, 0), turned)
        r["local"][q] = jnp.where(row8 < 6, turned[0:8, :], turned[rows - 8 : rows, :])
    goal = iota((lanes, 128), 1)
    cell = jnp.where(goal < mid.z + W, goal, goal - 128)
    cell = (cell + 128) // 2 - 64
    wanted = (goal < mid.z + W) | (goal >= 128 - W)
    matrix = jnp.where((iota((lanes, 128), 0) == 32 * at["gz"] + cell) & wanted, 1.0, 0.0).astype(F32)
    spread = dot(r["local"][...].reshape(64, lanes), matrix).reshape(8, 8, 128)
    E1 = r["E1"]
    for q in range(8):
        r["wide"][pl.ds(0, 8, stride=2), :] = spread[q]
        r["wide"][pl.ds(1, 8, stride=2), :] = spread[q]
        for k in range(2):
            x = 2 * q + k
            E1[x] = jnp.where(K1[x] > 0.0, E1[x] + r["wide"][...], 0.0)
    for reach, colour in ((3, 0), (2, 1), (1, 0), (0, 1)):
        half_sweep(mid, E1, g1, faces1, iv1, colour, reach)

    matrix = jnp.where(iota((128, 128), 0) == iota((128, 128), 1) // 2, 1.0, 0.0).astype(F32)
    fresh = dot(E1[W : W + mid.x, 0 : mid.y, :].reshape(mid.x * mid.y, 128), matrix).reshape(mid.x, mid.y, 128)
    Q0 = r["Q0"]
    for i in range(mid.x):
        r["wide"][pl.ds(0, mid.y, stride=2), :] = fresh[i]
        r["wide"][pl.ds(1, mid.y, stride=2), :] = fresh[i]
        for k in range(2):
            x = W + 2 * i + k
            Q0[x, 0 : fine.y, 0:128] = v0[x, 0 : fine.y, 0:128] + r["wide"][...]
    drain(exchange(fine, Q0, bufs(2, ""), counts))
    for reach, colour in ((3, 0), (2, 1), (1, 0), (0, 1)):
        half_sweep(fine, Q0, g0, faces0, iv0, colour, reach)
    out[...] = Q0[W : W + fine.x, 0 : fine.y, 0:128]


def per_device(counts, old_slots, old_ids, old_owner, coefficient):
    x, y, z = coefficient.shape
    fine, mid = Level(x, y, z), Level(x // 2, y // 2, z // 2)
    planes, rows, lanes = 4 * counts["gx"], 4 * counts["gy"], 32 * counts["gz"]
    groups, boxes = counts["gz"], z // BOX
    cells = old_slots.shape[3]
    partners = counts["gx"] - 1 + counts["gy"] * groups - 1
    vmem = lambda *shape: pltpu.VMEM(shape, F32)
    dma = lambda *shape: pltpu.SemaphoreType.DMA(shape)
    scratch = {}
    for level, tail, names in ((fine, "", ("K0", "P0", "Q0")), (mid, "m", ("K1", "P1", "E1"))):
        for name in names:
            scratch[name] = vmem(*level.shape)
        scratch["py" + tail] = vmem(3, 2, level.x, W, 128)
        scratch["ly" + tail] = vmem(3, 2, level.xe, W, 128)
        scratch["pz" + tail] = vmem(3, level.y, 128)
        scratch["lz" + tail] = vmem(3, 2, 3, 3, level.y, 128)
        scratch["es" + tail] = dma(3, len(NEAR))
        scratch["er" + tail] = dma(3, len(NEAR))
        scratch["pairs" + tail] = vmem(level.x // 2, level.y, 128)
    for level, tail in ((fine, "0"), (mid, "1")):
        for name in ("fx", "fy", "fz", "dd", "iv", "v", "g"):
            scratch[name + tail] = vmem(*level.shape)
    scratch.update(
        outgoing=vmem(groups, SEND, cells), incoming=vmem(groups, SEND, cells), ms=dma(groups - 1), mr=dma(groups - 1),
        lhs=pltpu.VMEM((BOX * BOX, boxes * BOX * BOX), jnp.bfloat16),
        rhs=pltpu.VMEM((boxes * BOX * BOX, 128), jnp.bfloat16),
        tmp=vmem(mid.y, 128), wide=vmem(16, 128), local=vmem(8, 8, lanes),
        gk=vmem(counts["gx"], counts["gy"], groups, 8, 128), gf=vmem(counts["gx"], counts["gy"], groups, 8, 128),
        gs=dma(2, partners), gr=dma(2, partners),
        f2=vmem(planes + 2, rows, lanes), k2=vmem(planes + 2, rows, lanes), s2=vmem(planes + 2, rows, lanes),
        v2=vmem(planes, rows, lanes), x2=vmem(planes + 4, rows, lanes))
    return pl.pallas_call(
        functools.partial(kernel, fine, mid, counts, tuple(scratch)),
        out_shape=jax.ShapeDtypeStruct(coefficient.shape, F32),
        in_specs=[pl.BlockSpec(memory_space=pltpu.VMEM)] * 4,
        out_specs=pl.BlockSpec(memory_space=pltpu.VMEM),
        scratch_shapes=list(scratch.values()),
        compiler_params=pltpu.CompilerParams(
            collective_id=0, has_side_effects=True, vmem_limit_bytes=60 * 1024 * 1024),
    )(old_slots, old_ids, old_owner, coefficient)


def solution(mesh):
    counts = {axis: mesh.shape[axis] for axis in ("gx", "gy", "gz")}
    return jax.shard_map(
        functools.partial(per_device, counts), mesh=mesh,
        in_specs=(P("gx", "gy", "gz", None), P("gx", "gy", "gz"), P("gx", "gy", None), P("gx", "gy", "gz")),
        out_specs=P("gx", "gy", "gz"), check_vma=False)
```

profile of v0, /device:TPU:0, one launch (start us, length us, event | category | flops | bytes accessed | tf_op | source)
XLA Modules:
  0.0 49.5 jit_solution(7582736062175290072)
XLA Ops:
  0.0 48.0 %shard_map.46 = f32[16,16,128]{2,1,0:T(8,128)} custom-call(bf16[1,1,8,4096]{3,2,1,0:T(8,128)(2,1)} %slots.1, s32[1,1,8]{2,1,0:T(1,128)} %ids.1, s32[1,1,32]{2,1,0:T(1,128)} %owner.1, f32[16,16,128]{2,1,0:T(8,128)} %coef.1), custom_call_target="tpu_custom_call" | custom-call | tf_op jit(solution)/shard_map/pallas_call | solution.py:562
  48.0 1.6 %copy.6 = f32[16,16,128]{2,1,0:T(8,128)} copy(f32[16,16,128]{2,1,0:T(8,128)} %shard_map.46) | data formatting | bytes 262144
where the time goes:
time: 49.7 us; the launch traced here: 49.5 us
  Pallas kernels  48 us (97%)
  local copies, waits for them, and re-layouts  1.57 us (3%)
    pallas_call x1, Pallas kernels, per_device(): pl.pallas_call(functools.partial(kernel, fine, mid, counts, tuple(scratch...  48 us
    unnamed x1, local copies, waits for them, and re-layouts  1.57 us

commit v1 on v0

v1 whole, which is shorter than its diff:
```python
import functools
import itertools

import jax
import jax.numpy as jnp
from jax import lax
from jax.experimental import pallas as pl
from jax.experimental.pallas import tpu as pltpu
from jax.sharding import PartitionSpec as P

BOX = 16
SEND = 2
F32 = jnp.float32
BF16 = jnp.bfloat16
MESH = pl.DeviceIdType.MESH
HIGH = lax.Precision.HIGHEST


def iota(shape, dim):
    return lax.broadcasted_iota(jnp.int32, shape, dim)


def up(v, axis):
    return pltpu.roll(v, 1, axis)


def down(v, axis):
    return pltpu.roll(v, v.shape[axis] - 1, axis)


class Level:
    def __init__(self, x, y, z, w, deep=False):
        self.x, self.y, self.z, self.w, self.deep = x, y, z, w, deep
        self.wx, self.wy = w + deep, -(-w // 4) * 4
        self.xe, self.ye = x + 2 * self.wx, y + 2 * self.wy
        self.ze = 128 if z + 2 * w <= 128 else z + 128
        self.shape = (self.xe, self.ye, self.ze)
        self.blocks = y // self.wy

    def units(self, a, b, c):
        extra = self.x // 4 if self.deep and not a and (not b or not c) else 0
        if c:
            return (self.wy if b else self.y) // 4 + extra
        return (self.wx if a else self.x) * (self.wy if b else self.y) // 4 + extra


NEAR = [(a, b, c) for c in (-1, 0, 1) for b in (-1, 0, 1) for a in (-1, 0, 1) if (a, b, c) != (0, 0, 0)]


def near(offset, counts):
    target, exists = {}, None
    for axis, step in zip(("gx", "gy", "gz"), offset):
        me, n = lax.axis_index(axis), counts[axis]
        if step:
            target[axis] = lax.rem(me + step + n, n)
            inside = me > 0 if step < 0 else me < n - 1
            exists = inside if exists is None else jnp.logical_and(exists, inside)
    return target, exists


def wait_units(units, count, sem):
    part = units.at[pl.ds(0, count)]
    pltpu.make_async_copy(part, part, sem).wait()


def wait_near(lv, counts, units, sems):
    choices = []
    for axis in ("gx", "gy", "gz"):
        me, n = lax.axis_index(axis), counts[axis]
        if n == 1:
            choices.append([(0, None)])
        elif n == 2:
            choices.append([(1, None)])
        else:
            edge = jnp.logical_or(me == 0, me == n - 1)
            choices.append([(1, edge), (2, jnp.logical_not(edge))])
    for chosen in itertools.product(*choices):
        total = 0
        for kind in itertools.product((0, 1), repeat=3):
            if any(kind):
                copies = 1
                for used, (number, _) in zip(kind, chosen):
                    copies *= number if used else 1
                total += copies * lv.units(*kind)
        conditions = [condition for _, condition in chosen if condition is not None]

        def wait():
            for sem in sems:
                wait_units(units, total, sem)

        if conditions:
            pl.when(functools.reduce(jnp.logical_and, conditions))(wait)
        else:
            wait()


def pack_sides(lv, v, bufs, deep=None):
    py, ly, pz, lz, lzb = bufs
    own, w = slice(lv.wx, lv.wx + lv.x), lv.w
    if lv.blocks > 1:
        py[0] = v[own, 0 : lv.wy, 0:128]
        py[1] = v[own, lv.y - lv.wy : lv.y, 0:128]
    lane = iota((lv.y, 128), 1)
    packed = layer = jnp.zeros((lv.y, 128), F32)
    for k in range(lv.x):
        plane = v[lv.wx + k, 0 : lv.y, 0:128]
        if lv.z == 64:
            plane = jnp.where(lane >= 64, pltpu.roll(plane, 64, 1), plane)
        turned = pltpu.roll(plane, (2 * w * k + w) % 128, 1)
        packed = jnp.where(lane // (2 * w) == k, turned, packed)
        if deep:
            layer = jnp.where((lane == (2 * w * k - 1) % 128) | (lane == (2 * w * k + 2 * w) % 128), turned, layer)
            deep[0][0, k : k + 1, :] = plane[w : w + 1, :]
            deep[0][1, k : k + 1, :] = plane[lv.y - w - 1 : lv.y - w, :]
    if deep:
        deep[2][...] = layer
    for block in range(lv.blocks):
        pz[block] = packed[block * lv.wy : block * lv.wy + lv.wy]


def send_sides(lv, v, bufs, sems, counts, deep=None):
    py, ly, pz, lz, lzb = bufs
    wx, block = lv.wx, (pl.ds(0, lv.y), pl.ds(0, 128))
    taken = {-1: (0, wx), 0: (0, lv.x), 1: (lv.x - wx, wx)}
    landed = {-1: lv.x + wx, 0: wx, 1: 0}
    for a, b, c in reversed(sorted(NEAR, key=lambda n: (n[0] != 0) + (n[1] != 0) + (n[2] != 0))):
        target, exists = near((a, b, c), counts)
        first, count = taken[a]
        if c and b:
            src, dst = pz.at[0 if b < 0 else lv.blocks - 1], lzb.at[(1 - c) // 2, 1 - a, (1 - b) // 2]
        elif c:
            src, dst = pz, lz.at[(1 - c) // 2, 1 - a]
        elif b:
            side = (b + 1) // 2
            src = py.at[side, pl.ds(first, count)] if lv.blocks > 1 else v.at[(pl.ds(wx + first, count),) + block]
            dst = ly.at[side, pl.ds(landed[a], count)]
        else:
            src, dst = v.at[(pl.ds(wx + first, count),) + block], v.at[(pl.ds(landed[a], count),) + block]
        copy = pltpu.make_async_remote_copy(
            src, dst, sems.at[0], sems.at[1], device_id=target, device_id_type=MESH)
        pl.when(exists)(copy.start)
        if deep and not a and (not b or not c):
            src, dst = (deep[2], deep[3].at[(1 - c) // 2]) if c else (deep[0].at[side], deep[1].at[side])
            copy = pltpu.make_async_remote_copy(
                src, dst, sems.at[0], sems.at[1], device_id=target, device_id_type=MESH)
            pl.when(exists)(copy.start)


def take_sides(lv, v, bufs, sems, counts, units, deep=None):
    py, ly, pz, lz, lzb = bufs
    w, wx = lv.w, lv.wx
    wait_near(lv, counts, units, (sems.at[0], sems.at[1]))
    v[:, lv.y : lv.y + lv.wy, 0:128] = ly[0]
    v[:, lv.y + lv.wy : lv.ye, 0:128] = ly[1]
    side = iota((lv.ye, 128), 1)
    edge = (side < w) | (side >= 128 - w)
    for a in range(3):
        parts = []
        for c in range(2):
            rows = [lz[c, a, block] for block in range(lv.blocks)]
            parts.append(jnp.concatenate(rows + [lzb[c, a, 1], lzb[c, a, 0]], axis=0))
        both = jnp.where(side % (2 * w) >= w, parts[1], parts[0])
        first = (0, wx, lv.x + wx)[a]
        start, count = ((lv.x - wx, wx), (0, lv.x), (0, wx))[a]
        for k in range(count):
            x = first + k
            strip = jnp.where(edge, pltpu.roll(both, (-2 * w * (start + k) - w) % 128, 1), 0.0)
            if lv.z == 64:
                v[x] = jnp.where(side < 64, v[x], jnp.where(side >= 128 - w, strip, pltpu.roll(strip, 64, 1)))
            else:
                v[x, :, lv.z : lv.z + 128] = strip
            if deep and a == 1:
                lane = iota((lv.y, 128), 1)
                layer = jnp.where(lane % (2 * w) == 2 * w - 1, deep[3][0], deep[3][1])
                layer = pltpu.roll(layer, (-2 * w * k - w) % 128, 1)
                edge5 = (lane == w) | (lane == 127 - w)
                v[x, 0 : lv.y, lv.z : lv.z + 128] = jnp.where(edge5, layer, strip[0 : lv.y])


def gather_start(buf, sems, counts):
    me = {axis: lax.axis_index(axis) for axis in counts}
    mine = buf.at[me["gx"], me["gy"], me["gz"]]
    ranges = [[n - k if k else 0 for k in range(n)] for n in counts.values()]
    for offset in sorted(itertools.product(*ranges), key=lambda o: -sum(1 for k in o if k)):
        if any(offset):
            target = {axis: lax.rem(me[axis] + k, counts[axis]) for axis, k in zip(counts, offset) if k}
            pltpu.make_async_remote_copy(
                mine, mine, sems.at[0], sems.at[1], device_id=target, device_id_type=MESH).start()


def gather_wait(sems, counts, units):
    others = counts["gx"] * counts["gy"] * counts["gz"] - 1
    if others:
        wait_units(units, others, sems.at[0])
        wait_units(units, others, sems.at[1])


def batches(low, high, size, body):
    whole = (high - low) // size
    if whole:
        def run(step, carry):
            body(low + step * size, size)
            return carry

        lax.fori_loop(0, whole, run, 0)
    if low + whole * size < high:
        body(low + whole * size, high - low - whole * size)


def prepare(lv, k, fx, fy, fz, dd, iv, off=0, rows=None):
    row = iota((lv.ye, lv.ze), 0)

    def body(first, count, inside=False):
        made = []
        for x in [first + i for i in range(count)]:
            kx = k[x + off]
            below = 0.5 * ((k[x + off - 1] if off else k[jnp.maximum(x - 1, 0)]) + kx)
            above = 0.5 * (kx + (k[x + off + 1] if off else k[jnp.minimum(x + 1, lv.xe - 1)]))
            lower, upper = up(kx, 0), down(kx, 0)
            if inside:
                side = jnp.zeros((lv.ye, lv.ze - 128), F32)
                ends = [jnp.broadcast_to(rows[b, pl.ds(x - lv.w, 1), :], (lv.ye, 128)) for b in range(2)]
                ends = [jnp.concatenate([end, side], axis=1) for end in ends]
                upper = jnp.where(row == lv.y + lv.wy - 1, ends[0], upper)
                lower = jnp.where(row == lv.y + lv.wy, ends[1], lower)
            second = 0.5 * (lower + kx)
            third = 0.5 * (up(kx, 1) + kx)
            total = below + above + second + 0.5 * (kx + upper) + third + down(third, 1)
            made.append((x, below, second, third, total, jnp.where(kx > 0.0, 1.0 / total, 0.0)))
        for x, *values in made:
            for ref, value in zip((fx, fy, fz, dd, iv), values):
                ref[x] = value

    size = 4 if lv.ze == 128 else 2
    if rows is None:
        batches(0, lv.xe, size, body)
    else:
        batches(0, lv.w, size, body)
        batches(lv.w, lv.w + lv.x, size, functools.partial(body, inside=True))
        batches(lv.w + lv.x, lv.xe, size, body)


def around(v, x, mid, faces):
    fx, fy, fz = faces
    second, third = fy[x], fz[x]
    summed = fx[x] * v[x - 1] + fx[x + 1] * v[x + 1]
    summed = summed + second * up(mid, 0) + down(second * mid, 0)
    return summed + third * up(mid, 1) + down(third * mid, 1)


def half_sweep(lv, v, g, faces, iv, colour, reach):
    parity = iota((lv.ye, lv.ze), 0) + iota((lv.ye, lv.ze), 1)

    def body(first, count):
        fresh = []
        for x in [first + i for i in range(count)]:
            mid = v[x]
            value = (g[x] + around(v, x, mid, faces)) * iv[x]
            fresh.append((x, jnp.where(((parity + x) & 1) == colour, value, mid)))
        for x, value in fresh:
            v[x] = value

    batches(lv.w - reach, lv.w + lv.x + reach, 10 if lv.ze == 128 else 6, body)


def residual_pairs(lv, v, g, faces, dd, pairs):
    def body(first, count):
        made = []
        for i in [first + j for j in range(count)]:
            total = jnp.zeros((lv.ye, lv.ze), F32)
            for k in range(2):
                x = lv.w + 2 * i + k
                mid = v[x]
                total = total + (g[x] - dd[x] * mid + around(v, x, mid, faces))
            made.append((i, total))
        for i, total in made:
            pairs[i] = total[0 : lv.y, 0:128]

    batches(0, lv.x // 2, 4, body)


def open_halo(lv, v, g, iv):
    parity = iota((lv.ye, lv.ze), 0) + iota((lv.ye, lv.ze), 1)

    def body(first, count):
        made = []
        for x in [first + i for i in range(count)]:
            made.append((x, jnp.where(((parity + x) & 1) == 0, g[x] * iv[x], 0.0)))
        for x, value in made:
            v[x] = value

    batches(lv.w - 4, lv.w + lv.x + 4, 4, body)


def fold_rows(pairs, rows):
    return pairs[:, pl.ds(0, rows, stride=2), :] + pairs[:, pl.ds(1, rows, stride=2), :]


def dot(a, b):
    return jnp.dot(a, b, precision=HIGH, preferred_element_type=F32)


def coarse_mid(pairs, x, y):
    folded = fold_rows(pairs, y // 2).reshape((x // 2) * (y // 2), 128)
    matrix = jnp.where(iota((128, 128), 0) // 2 == iota((128, 128), 1), 0.125, 0.0).astype(F32)
    return dot(folded, matrix).reshape(x // 2, y // 2, 128)


def coarse_low(pairs, count, rows, lanes, tmp):
    total = jnp.zeros((rows, 128), F32)
    source, goal = iota((128, 128), 0), iota((128, 128), 1)
    for x in range(count):
        matrix = jnp.where((source // 2 + x * lanes == goal) & (source < 2 * lanes), 0.125, 0.0).astype(F32)
        total = total + dot(pairs[x], matrix)
    tmp[...] = total
    half = rows // 2
    return tmp[pl.ds(0, half, stride=2), :] + tmp[pl.ds(1, half, stride=2), :]


def repeat(count, body, carry):
    if count <= 16:
        for p in range(count):
            carry = body(p, carry)
        return carry
    return lax.fori_loop(0, count, body, carry)


def spread_low(buf, whole, counts, pad):
    lane = iota((8, 128), 1)

    def body(a, carry):
        for ct in range(counts["gy"] // 2):
            for gt in range(counts["gz"] // 4):
                pieces = [
                    jnp.concatenate([buf[a, 2 * ct, 4 * gt + g], buf[a, 2 * ct + 1, 4 * gt + g]], axis=0)
                    for g in range(4)]
                for i in range(4):
                    total = pieces[0] if i == 0 else pltpu.roll(pieces[0], (-32 * i) % 128, 1)
                    for g in range(1, 4):
                        piece = pieces[g] if g == i else pltpu.roll(pieces[g], (32 * (g - i)) % 128, 1)
                        total = jnp.where(lane // 32 == g, piece, total)
                    whole[pad + 4 * a + i, 8 * ct : 8 * ct + 8, 128 * gt : 128 * gt + 128] = total
        return carry

    repeat(counts["gx"], body, 0)


def low_faces(k, faces, dims, pad):
    planes, rows, lanes = dims
    cx, cy0, cy1, cz0, cz1, cd = faces
    row, lane = iota((rows, lanes), 0), iota((rows, lanes), 1)
    scale = 0.5 * 0.0625

    def body(p, carry):
        kx = k[p + pad]
        below, above = scale * (k[p + pad - 1] + kx), scale * (kx + k[p + pad + 1])
        total = below + above
        cx[p] = below
        cx[p + 1] = above
        for target, inside, moved in (
            (cy0, row > 0, up(kx, 0)), (cy1, row < rows - 1, down(kx, 0)),
            (cz0, lane > 0, up(kx, 1)), (cz1, lane < lanes - 1, down(kx, 1))):
            face = scale * (kx + moved)
            target[p] = jnp.where(inside, face, 0.0)
            total = total + jnp.where(inside, face, scale * kx)
        cd[p] = total
        return carry

    repeat(planes, body, 0)


def bottom(f, s, vv, faces, dims, pad):
    planes, rows, lanes = dims
    cx, cy0, cy1, cz0, cz1, cd = faces

    def operate(v, p):
        mid = v[p + pad]
        summed = cx[p] * v[p + pad - 1] + cx[p + 1] * v[p + pad + 1]
        summed = summed + (cy0[p] * up(mid, 0) + cy1[p] * down(mid, 0))
        summed = summed + (cz0[p] * up(mid, 1) + cz1[p] * down(mid, 1))
        return mid, cd[p] * mid - summed

    zero = jnp.zeros((rows, lanes), F32)

    def first(p, carry):
        mid, image = operate(f, p)
        vv[p] = image
        return carry[0] + mid * mid, carry[1] + mid * image

    def total(v):
        return jnp.sum(jnp.sum(v, axis=0, keepdims=True), axis=1, keepdims=True)

    norm, along = repeat(planes, first, (zero, zero))
    alpha = total(norm) / total(along)

    def rest(p, carry):
        s[p + pad] = f[p + pad] - alpha * vv[p]
        return carry

    repeat(planes, rest, 0)

    def second(p, carry):
        mid, image = operate(s, p)
        return carry[0] + image * mid, carry[1] + image * image

    turned, norm = repeat(planes, second, (zero, zero))
    return alpha, total(turned) / total(norm)


def pack_boxes(slots, ids, outgoing, boxes, groups):
    held = ids[0].astype(F32)
    cap = held.shape[1]
    eye = iota((cap, cap), 0) == iota((cap, cap), 1)
    rows = jnp.broadcast_to(held, (cap, cap))
    cols = jnp.broadcast_to(jnp.sum(jnp.where(eye, rows, 0.0), axis=1, keepdims=True), (cap, cap))

    def target(v):
        return jnp.floor((v + 0.5) * (1.0 / boxes))

    earlier = (target(rows) == target(cols)) & (cols < rows) & (cols >= 0.0)
    ranking = jnp.sum(jnp.where(earlier, 1.0, 0.0), axis=0, keepdims=True)
    send_row = jnp.where(held >= 0.0, target(held) * SEND + ranking, -1.0)
    count = groups * SEND
    picker = jnp.where(iota((count, cap), 0).astype(F32) == jnp.broadcast_to(send_row, (count, cap)), 1.0, 0.0)
    data = slots[0, 0].astype(F32)
    total = jnp.zeros((count, data.shape[1]), F32)
    for q in range(cap):
        total = total + picker[:, q : q + 1] * data[q : q + 1, :]
    for t in range(groups):
        outgoing[t] = total[SEND * t : SEND * t + SEND, :].astype(BF16)


def place_boxes(incoming, held, owner, lhs, rhs, boxes, groups):
    me = lax.axis_index("gz")
    owners = jnp.broadcast_to(owner[0].astype(F32), (boxes, owner.shape[2]))
    here = iota(owners.shape, 1) == iota(owners.shape, 0) + me * boxes
    col = jnp.sum(jnp.where(here, owners, 0.0), axis=1, keepdims=True)
    cols = jnp.broadcast_to(col, (boxes, boxes))
    first, second = iota((boxes, boxes), 0), iota((boxes, boxes), 1)
    row = jnp.sum(jnp.where(first == second, cols, 0.0), axis=0, keepdims=True)
    before = (jnp.broadcast_to(row, (boxes, boxes)) == cols) & (second < first)
    pick = col * SEND + jnp.sum(jnp.where(before, 1.0, 0.0), axis=1, keepdims=True)
    for t in range(groups):
        held[SEND * t : SEND * t + SEND, :] = incoming[t].astype(F32)
    face = BOX * BOX
    mine = iota((BOX, face), 1) // BOX == iota((BOX, face), 0)
    for i in range(BOX):
        chosen = jnp.zeros((boxes, face), F32)
        for r in range(groups * SEND):
            chosen = jnp.where(pick == float(r), held[r : r + 1, face * i : face * i + face], chosen)
        for b in range(boxes):
            piece = jnp.where(mine, jnp.broadcast_to(chosen[b : b + 1, :], (BOX, face)), 0.0)
            lhs[BOX * i : BOX * i + BOX, face * b : face * b + face] = piece.astype(BF16)
    return jnp.dot(lhs[...], rhs[...], preferred_element_type=F32)


def kernel(fine, edge, mid, counts, names, slots_in, ids_in, owner_in, coef_in, out, *scratch):
    r = dict(zip(names, scratch))
    groups = counts["gz"]
    boxes = fine.z // BOX
    at = {axis: lax.axis_index(axis) for axis in counts}
    slots, ids, owner, coef, units = r["slots"], r["ids"], r["owner"], r["coef"], r["units"]
    loads = [
        pltpu.make_async_copy(source, target, r["loads"].at[n])
        for n, (source, target) in enumerate(((slots_in, slots), (ids_in, ids), (coef_in, coef), (owner_in, owner)))]
    for load in loads:
        load.start()
    for name in ("K0", "F0", "Q0", "K1", "G1", "E1", "lyk", "ly", "lz", "lzb", "lym", "lzm", "lzbm", "kyl", "kzl"):
        r[name][...] = jnp.zeros(r[name].shape, F32)

    barrier = pltpu.get_barrier_semaphore()
    expected = 0
    for offset in NEAR:
        target, exists = near(offset, counts)

        @pl.when(exists)
        def _():
            pl.semaphore_signal(barrier, inc=1, device_id=target, device_id_type=MESH)

        expected = expected + jnp.where(exists, 1, 0)
    others = [{"gz": lax.rem(at["gz"] + k, groups)} for k in range(1, groups)]
    if counts["gx"] > 4 or counts["gy"] > 4:
        for offset in itertools.product(*[range(n) for n in counts.values()]):
            if any(offset):
                others.append({axis: lax.rem(at[axis] + k, counts[axis]) for axis, k in zip(counts, offset) if k})
    for target in others:
        pl.semaphore_signal(barrier, inc=1, device_id=target, device_id_type=MESH)

    def bufs(n, tail):
        return tuple(r[b + tail].at[n] for b in ("py", "ly", "pz", "lz", "lzb"))

    def edge_bufs():
        return tuple(r[b + "k"].at[0] if b == "ly" else r[b].at[0] for b in ("py", "ly", "pz", "lz", "lzb"))

    def sems(n):
        return r["sems"].at[n]

    loads[0].wait()
    loads[1].wait()
    pack_boxes(slots, ids, r["outgoing"], boxes, groups)
    K0, F0, Q0, K1, G1, E1 = (r[name] for name in ("K0", "F0", "Q0", "K1", "G1", "E1"))
    w, wm = fine.w, mid.w
    loads[2].wait()
    K0[edge.wx : edge.wx + fine.x, 0 : fine.y, 0:128] = coef[...]
    deep = tuple(r[name] for name in ("kys", "kyl", "kzs", "kzl"))
    pack_sides(edge, K0, edge_bufs(), deep)
    pl.semaphore_wait(barrier, expected + len(others))

    me = at["gz"]
    for k in range(1, groups):
        to = lax.rem(me + k, groups)
        pltpu.make_async_remote_copy(
            r["outgoing"].at[to], r["incoming"].at[me], sems(0).at[0], sems(0).at[1],
            device_id={"gz": to}, device_id_type=MESH).start()
    send_sides(edge, K0, edge_bufs(), sems(1), counts, deep)
    r["incoming"][me] = r["outgoing"][me]

    for i in range(mid.x):
        r["pairs"][i] = coef[2 * i] + coef[2 * i + 1]
    K1[wm : wm + mid.x, 0 : mid.y, :] = coarse_mid(r["pairs"], fine.x, fine.y)
    pack_sides(mid, K1, bufs(0, "m"))
    send_sides(mid, K1, bufs(0, "m"), sems(2), counts)
    for i in range(mid.x // 2):
        r["pairsm"][i] = K1[wm + 2 * i, 0 : mid.y, :] + K1[wm + 2 * i + 1, 0 : mid.y, :]
    here = (at["gx"], at["gy"], at["gz"])
    r["gk"][here] = coarse_low(r["pairsm"], mid.x // 2, mid.y, mid.z // 2, r["tmp"])
    lane = iota((BOX * BOX, 128), 1)
    folded = iota((BOX * BOX, 128), 0) % BOX == lane % BOX
    for b in range(boxes):
        block = jnp.where(folded & (lane // BOX == b), 1.0, 0.0)
        r["rhs"][BOX * BOX * b : BOX * BOX * (b + 1), :] = block.astype(BF16)
    loads[3].wait()
    if groups > 1:
        part = r["incoming"].at[pl.ds(0, groups - 1)]
        for n in range(2):
            pltpu.make_async_copy(part, part, sems(0).at[n]).wait()
    source = place_boxes(r["incoming"], r["held"], owner, r["lhs"], r["rhs"], boxes, groups)
    F0[w : w + fine.x, 0 : fine.y, 0:128] = source.reshape(fine.x, fine.y, 128)
    pack_sides(fine, F0, bufs(1, ""))
    send_sides(fine, F0, bufs(1, ""), sems(3), counts)

    faces0 = (r["fx0"], r["fy0"], r["fz0"])
    faces1 = (r["fx1"], r["fy1"], r["fz1"])
    dd0, iv0, dd1, iv1, v0, v1 = r["dd0"], r["iv0"], r["dd1"], r["iv1"], r["v0"], r["v1"]
    take_sides(edge, K0, edge_bufs(), sems(1), counts, units, deep)
    prepare(fine, K0, *faces0, dd0, iv0, edge.wx - w, r["kyl"])
    take_sides(mid, K1, bufs(0, "m"), sems(2), counts, units)
    prepare(mid, K1, *faces1, dd1, iv1)
    for name in ("k2", "f2", "s2"):
        r[name][...] = jnp.zeros(r[name].shape, F32)
    take_sides(fine, F0, bufs(1, ""), sems(3), counts, units)
    open_halo(fine, v0, F0, iv0)
    for reach, colour in ((3, 1), (2, 0), (1, 1)):
        half_sweep(fine, v0, F0, faces0, iv0, colour, reach)
    residual_pairs(fine, v0, F0, faces0, dd0, r["pairs"])

    G1[wm : wm + mid.x, 0 : mid.y, :] = 4.0 * coarse_mid(r["pairs"], fine.x, fine.y)
    pack_sides(mid, G1, bufs(1, "m"))
    send_sides(mid, G1, bufs(1, "m"), sems(4), counts)
    Q0[w : w + fine.x, 0 : fine.y, 0:128] = v0[w : w + fine.x, 0 : fine.y, 0:128]
    pack_sides(fine, Q0, bufs(2, ""))
    send_sides(fine, Q0, bufs(2, ""), sems(5), counts)
    take_sides(mid, G1, bufs(1, "m"), sems(4), counts, units)
    gather_start(r["gk"], sems(7), counts)
    open_halo(mid, v1, G1, iv1)
    for reach, colour in ((3, 1), (2, 0), (1, 1)):
        half_sweep(mid, v1, G1, faces1, iv1, colour, reach)
    residual_pairs(mid, v1, G1, faces1, dd1, r["pairsm"])
    for i in range(mid.x // 2):
        r["pairsm"][i] = r["pairsm"][i] * 0.25
    r["gf"][here] = coarse_low(r["pairsm"], mid.x // 2, mid.y, mid.z // 2, r["tmp"])
    gather_start(r["gf"], sems(8), counts)
    E1[wm : wm + mid.x, 0 : mid.y, :] = v1[wm : wm + mid.x, 0 : mid.y, :]
    pack_sides(mid, E1, bufs(2, "m"))
    send_sides(mid, E1, bufs(2, "m"), sems(6), counts)

    planes, rows, lanes = dims = (4 * counts["gx"], 4 * counts["gy"], 32 * counts["gz"])
    pad = wm // 2
    low = tuple(r[name] for name in ("cx", "cy0", "cy1", "cz0", "cz1", "cd"))
    take_sides(fine, Q0, bufs(2, ""), sems(5), counts, units)
    gather_wait(sems(7), counts, units)
    spread_low(r["gk"], r["k2"], counts, pad)
    low_faces(r["k2"], low, dims, pad)
    take_sides(mid, E1, bufs(2, "m"), sems(6), counts, units)
    gather_wait(sems(8), counts, units)
    spread_low(r["gf"], r["f2"], counts, pad)
    alpha, omega = bottom(r["f2"], r["s2"], r["v2"], low, dims, pad)
    around_low = mid.xe // 2
    for q in range(around_low):
        turned = alpha * r["f2"][4 * at["gx"] + q] + omega * r["s2"][4 * at["gx"] + q]
        plane = turned
        for c in range(1, counts["gy"]):
            turned = jnp.where(at["gy"] == c, pltpu.roll(plane, rows - 4 * c, 0), turned)
        r["local"][q, 0:8, :] = turned[0:8, :]
        r["local"][q, 8:16, :] = pltpu.roll(turned[rows - 8 : rows, :], 4, 0)
    goal = iota((lanes, 128), 1)
    cell = jnp.where(goal < mid.z + wm, goal, goal - 128)
    cell = (cell + 128) // 2 - 64
    wanted = (goal < mid.z + wm) | (goal >= 128 - wm)
    matrix = jnp.where((iota((lanes, 128), 0) == 32 * at["gz"] + cell) & wanted, 1.0, 0.0).astype(F32)
    spread = dot(r["local"][...].reshape(16 * around_low, lanes), matrix).reshape(around_low, 16, 128)
    for q in range(around_low):
        wide = r["wide"].at[q, 0]
        for k in range(2):
            wide[pl.ds(k, 12, stride=2), :] = spread[q, 0:12]
        for k in range(2):
            x = 2 * q + k
            E1[x] = jnp.where(K1[x] > 0.0, E1[x] + wide[...], 0.0)
    for reach, colour in ((5, 0), (4, 1), (3, 0), (2, 1)):
        half_sweep(mid, E1, G1, faces1, iv1, colour, reach)

    low_w = w // 2
    goal = iota((128, fine.ze), 1)
    cell = jnp.where(goal < fine.z + w, goal // 2, (goal - fine.ze + 256) // 2)
    wanted = (goal < fine.z + w) | (goal >= fine.ze - w)
    matrix = jnp.where((iota((128, fine.ze), 0) == cell) & wanted, 1.0, 0.0).astype(F32)
    used = mid.x + 2 * low_w
    row = iota((8, 128), 0)
    for i in range(used):
        x = wm - low_w + i
        r["turn"][i, 0:8, :] = E1[x, 0:8, :]
        r["turn"][i, 8:16, :] = jnp.where(row < low_w, E1[x, 8:16, :], pltpu.roll(E1[x, mid.ye - 8 : mid.ye, :], 4, 0))
    fresh = dot(r["turn"][...].reshape(16 * used, 128), matrix).reshape(used, 16, fine.ze)
    for i in range(used):
        for tile in range(fine.ze // 128):
            wide, part = r["wide"].at[i, tile], slice(128 * tile, 128 * tile + 128)
            for k in range(2):
                wide[pl.ds(k, 12, stride=2), :] = fresh[i, 0:12, part]
            for k in range(2):
                x = 2 * i + k
                Q0[x, :, part] = Q0[x, :, part] + wide[...]
    for reach, colour in ((3, 0), (2, 1), (1, 0), (0, 1)):
        half_sweep(fine, Q0, F0, faces0, iv0, colour, reach)
    out[...] = Q0[w : w + fine.x, 0 : fine.y, 0:128]


def per_device(counts, old_slots, old_ids, old_owner, coefficient):
    x, y, z = coefficient.shape
    fine, edge, mid = Level(x, y, z, 4), Level(x, y, z, 4, deep=True), Level(x // 2, y // 2, z // 2, 6)
    planes, rows, lanes = 4 * counts["gx"], 4 * counts["gy"], 32 * counts["gz"]
    groups, boxes = counts["gz"], z // BOX
    cells = old_slots.shape[3]
    pad = mid.w // 2
    devices = counts["gx"] * counts["gy"] * groups
    vmem = lambda *shape: pltpu.VMEM(shape, F32)
    dma = lambda *shape: pltpu.SemaphoreType.DMA(shape)
    scratch = {}
    for level, tail, names in ((fine, "", ("K0", "F0", "Q0")), (mid, "m", ("K1", "G1", "E1"))):
        for name in names:
            scratch[name] = vmem(*level.shape)
        scratch["py" + tail] = vmem(3, 2, level.x, level.wy, 128)
        scratch["ly" + tail] = vmem(3, 2, level.xe, level.wy, 128)
        scratch["pz" + tail] = vmem(3, level.blocks, level.wy, 128)
        scratch["lz" + tail] = vmem(3, 2, 3, level.blocks, level.wy, 128)
        scratch["lzb" + tail] = vmem(3, 2, 3, 2, level.wy, 128)
        scratch["pairs" + tail] = vmem(level.x // 2, level.y, 128)
    for level, tail in ((fine, "0"), (mid, "1")):
        for name in ("fx", "fy", "fz", "dd", "iv", "v"):
            scratch[name + tail] = vmem(*level.shape)
    scratch["K0"] = vmem(*edge.shape)
    scratch["lyk"] = vmem(1, 2, edge.xe, edge.wy, 128)
    scratch.update(
        kys=vmem(2, x, 128), kyl=vmem(2, x, 128), kzs=vmem(y, 128), kzl=vmem(2, y, 128),
        slots=pltpu.VMEM(old_slots.shape, old_slots.dtype), ids=pltpu.VMEM(old_ids.shape, old_ids.dtype),
        owner=pltpu.VMEM(old_owner.shape, old_owner.dtype), coef=vmem(*coefficient.shape), loads=dma(4),
        outgoing=pltpu.VMEM((groups, SEND, cells), BF16), incoming=pltpu.VMEM((groups, SEND, cells), BF16),
        held=vmem(groups * SEND, cells), sems=dma(9, 2), units=vmem(max(160, devices), 4, 128),
        lhs=pltpu.VMEM((BOX * BOX, boxes * BOX * BOX), BF16), rhs=pltpu.VMEM((boxes * BOX * BOX, 128), BF16),
        tmp=vmem(mid.y, 128), wide=vmem(max(mid.xe, fine.xe) // 2, fine.ze // 128, fine.ye, 128), local=vmem(mid.xe // 2, 16, lanes),
        turn=vmem(mid.x + fine.w, 16, 128),
        gk=vmem(counts["gx"], counts["gy"], groups, 4, 128), gf=vmem(counts["gx"], counts["gy"], groups, 4, 128),
        cx=vmem(planes + 1, rows, lanes), v2=vmem(planes, rows, lanes))
    for name in ("cy0", "cy1", "cz0", "cz1", "cd"):
        scratch[name] = vmem(planes, rows, lanes)
    for name in ("f2", "k2", "s2"):
        scratch[name] = vmem(planes + 2 * pad, rows, lanes)
    return pl.pallas_call(
        functools.partial(kernel, fine, edge, mid, counts, tuple(scratch)),
        out_shape=jax.ShapeDtypeStruct(coefficient.shape, F32),
        in_specs=[pl.BlockSpec(memory_space=pltpu.MemorySpace.HBM)] * 4,
        out_specs=pl.BlockSpec(memory_space=pltpu.VMEM),
        scratch_shapes=list(scratch.values()),
        compiler_params=pltpu.CompilerParams(
            collective_id=0, has_side_effects=True, vmem_limit_bytes=44 * 1024 * 1024),
    )(old_slots, old_ids, old_owner, coefficient)


def solution(mesh):
    counts = {axis: mesh.shape[axis] for axis in ("gx", "gy", "gz")}
    return jax.shard_map(
        functools.partial(per_device, counts), mesh=mesh,
        in_specs=(P("gx", "gy", "gz", None), P("gx", "gy", "gz"), P("gx", "gy", None), P("gx", "gy", "gz")),
        out_specs=P("gx", "gy", "gz"), check_vma=False)
```

time: 49.7 us -> 35.2 us (0.71)
  Pallas kernels: 48 us -> 31.3 us
  local copies, waits for them, and re-layouts: 1.57 us -> 3.71 us
    pallas_call x1, Pallas kernels: 48 us -> 31.3 us  [per_device(): pl.pallas_call(functools.partial(kernel, fine, edge, mid, counts, tuple(s...]
    unnamed x1 -> x9, local copies, waits for them, and re-layouts: 1.57 us -> 3.71 us
where the time goes in v1:
time: 35.2 us; the launch traced here: 35 us
  Pallas kernels  31.3 us (89%)
  local copies, waits for them, and re-layouts  3.71 us (11%)
    pallas_call x1, Pallas kernels, per_device(): pl.pallas_call(functools.partial(kernel, fine, edge, mid, counts, tuple(s...  31.3 us
    unnamed x9, local copies, waits for them, and re-layouts  3.71 us

profile of v1, /device:TPU:0, one launch (start us, length us, event | category | flops | bytes accessed | tf_op | source)
XLA Modules:
  0.0 35.0 jit_solution(3992615022200468190)
XLA Ops:
  0.0 0.0 copy-start
  0.0 0.9 %copy-done = f32[16,16,128]{2,1,0:T(8,128)S(1)} copy-done((f32[16,16,128]{2,1,0:T(8,128)S(1)}, f32[16,16,128]{2,1,0:T(8,128)}, u32[]{:S(2)}) %copy-start) | copy-done | bytes 131096
  0.9 0.0 copy-start.1
  0.9 0.8 %copy-done.1 = bf16[1,1,8,4096]{3,2,1,0:T(8,128)(2,1)S(1)} copy-done((bf16[1,1,8,4096]{3,2,1,0:T(8,128)(2,1)S(1)}, bf16[1,1,8,4096]{3,2,1,0:T(8,128)(2,1)}, u32[]{:S(2)}) %copy-start.1) | copy-done | bytes 65560
  1.7 0.0 copy-start.2
  1.7 0.7 %copy-done.2 = s32[1,1,8]{2,1,0:T(1,128)S(1)} copy-done((s32[1,1,8]{2,1,0:T(1,128)S(1)}, s32[1,1,8]{2,1,0:T(1,128)}, u32[]{:S(2)}) %copy-start.2) | copy-done | bytes 56
  2.4 0.0 copy-start.3
  2.4 0.7 %copy-done.3 = s32[1,1,32]{2,1,0:T(1,128)S(1)} copy-done((s32[1,1,32]{2,1,0:T(1,128)S(1)}, s32[1,1,32]{2,1,0:T(1,128)}, u32[]{:S(2)}) %copy-start.3) | copy-done | bytes 152
  3.1 31.3 %shard_map.46 = f32[16,16,128]{2,1,0:T(8,128)S(1)} custom-call(bf16[1,1,8,4096]{3,2,1,0:T(8,128)(2,1)S(1)} %copy-done.1, s32[1,1,8]{2,1,0:T(1,128)S(1)} %copy-done.2, s32[1,1,32]{2,1,0:T(1,128)S(1)} %copy-done.3, f32[16,16,128]{2,1,0:T(8,128)S(1)} %copy-done), custom_call_target="tpu_custom_call" | custom-call | tf_op jit(solution)/shard_map/pallas_call | solution.py:677
  34.3 0.7 %copy.6 = f32[16,16,128]{2,1,0:T(8,128)} copy(f32[16,16,128]{2,1,0:T(8,128)S(1)} %shard_map.46) | data formatting | bytes 262144
Async XLA Ops:
  0.0 0.9 %copy-start = (f32[16,16,128]{2,1,0:T(8,128)S(1)}, f32[16,16,128]{2,1,0:T(8,128)}, u32[]{:S(2)}) copy-start(f32[16,16,128]{2,1,0:T(8,128)} %coef_in.1) | copy-start | bytes 393220
  0.9 0.8 %copy-start.1 = (bf16[1,1,8,4096]{3,2,1,0:T(8,128)(2,1)S(1)}, bf16[1,1,8,4096]{3,2,1,0:T(8,128)(2,1)}, u32[]{:S(2)}) copy-start(bf16[1,1,8,4096]{3,2,1,0:T(8,128)(2,1)} %slots_in.1) | copy-start | bytes 196612
  1.7 0.7 %copy-start.2 = (s32[1,1,8]{2,1,0:T(1,128)S(1)}, s32[1,1,8]{2,1,0:T(1,128)}, u32[]{:S(2)}) copy-start(s32[1,1,8]{2,1,0:T(1,128)} %ids_in.1) | copy-start | bytes 100
  2.4 0.7 %copy-start.3 = (s32[1,1,32]{2,1,0:T(1,128)S(1)}, s32[1,1,32]{2,1,0:T(1,128)}, u32[]{:S(2)}) copy-start(s32[1,1,32]{2,1,0:T(1,128)} %owner_in.1) | copy-start | bytes 388

commit v2 on v1

--- a/solution.py
+++ b/solution.py
@@ -565,14 +565,14 @@
     open_halo(mid, v1, G1, iv1)
     for reach, colour in ((3, 1), (2, 0), (1, 1)):
         half_sweep(mid, v1, G1, faces1, iv1, colour, reach)
+    E1[wm : wm + mid.x, 0 : mid.y, :] = v1[wm : wm + mid.x, 0 : mid.y, :]
+    pack_sides(mid, E1, bufs(2, "m"))
+    send_sides(mid, E1, bufs(2, "m"), sems(6), counts)
     residual_pairs(mid, v1, G1, faces1, dd1, r["pairsm"])
     for i in range(mid.x // 2):
         r["pairsm"][i] = r["pairsm"][i] * 0.25
     r["gf"][here] = coarse_low(r["pairsm"], mid.x // 2, mid.y, mid.z // 2, r["tmp"])
     gather_start(r["gf"], sems(8), counts)
-    E1[wm : wm + mid.x, 0 : mid.y, :] = v1[wm : wm + mid.x, 0 : mid.y, :]
-    pack_sides(mid, E1, bufs(2, "m"))
-    send_sides(mid, E1, bufs(2, "m"), sems(6), counts)
 
     planes, rows, lanes = dims = (4 * counts["gx"], 4 * counts["gy"], 32 * counts["gz"])
     pad = wm // 2
@@ -682,7 +682,7 @@
         scratch_shapes=list(scratch.values()),
         compiler_params=pltpu.CompilerParams(
             collective_id=0, has_side_effects=True, vmem_limit_bytes=44 * 1024 * 1024),
-    )(old_slots, old_ids, old_owner, coefficient)
+    )(*[pltpu.with_memory_space_constraint(v, pltpu.HBM) for v in (old_slots, old_ids, old_owner, coefficient)])
 
 
 def solution(mesh):

time: 35.2 us -> 33 us (0.937)
  local copies, waits for them, and re-layouts: 3.71 us -> 0.66 us
  Pallas kernels: 31.3 us -> 32.2 us
    unnamed x9 -> x1, local copies, waits for them, and re-layouts: 3.71 us -> 0.66 us
    pallas_call x1, Pallas kernels: 31.3 us -> 32.2 us  [per_device(): pl.pallas_call(functools.partial(kernel, fine, edge, mid, counts, tuple(s...]
where the time goes in v2:
time: 33 us; the launch traced here: 32.9 us
  Pallas kernels  32.2 us (98%)
  local copies, waits for them, and re-layouts  0.66 us (2%)
    pallas_call x1, Pallas kernels, per_device(): pl.pallas_call(functools.partial(kernel, fine, edge, mid, counts, tuple(s...  32.2 us

profile of v2, /device:TPU:0, one launch (start us, length us, event | category | flops | bytes accessed | tf_op | source)
XLA Modules:
  0.0 32.9 jit_solution(3401634103379531498)
XLA Ops:
  0.0 32.2 %shard_map.46 = f32[16,16,128]{2,1,0:T(8,128)S(1)} custom-call(bf16[1,1,8,4096]{3,2,1,0:T(8,128)(2,1)} %slots_in.1, s32[1,1,8]{2,1,0:T(1,128)} %ids_in.1, s32[1,1,32]{2,1,0:T(1,128)} %owner_in.1, f32[16,16,128]{2,1,0:T(8,128)} %coef_in.1), custom_call_target="tpu_custom_call" | custom-call | tf_op jit(solution)/shard_map/pallas_call | solution.py:677
  32.2 0.7 %copy.6 = f32[16,16,128]{2,1,0:T(8,128)} copy(f32[16,16,128]{2,1,0:T(8,128)S(1)} %shard_map.46) | data formatting | bytes 262144

commit v3 on v2

v3 whole, which is shorter than its diff:
```python
import functools
import itertools

import jax
import jax.numpy as jnp
from jax import lax
from jax.experimental import pallas as pl
from jax.experimental.pallas import tpu as pltpu
from jax.sharding import PartitionSpec as P

BOX = 16
SEND = 2
F32 = jnp.float32
BF16 = jnp.bfloat16
MESH = pl.DeviceIdType.MESH
HIGH = lax.Precision.HIGHEST


def iota(shape, dim):
    return lax.broadcasted_iota(jnp.int32, shape, dim)


def up(v, axis):
    return pltpu.roll(v, 1, axis)


def down(v, axis):
    return pltpu.roll(v, v.shape[axis] - 1, axis)


class Level:
    def __init__(self, t, y, wt, wy, h, deep=False):
        self.t, self.y, self.wt, self.wy, self.h, self.deep = t, y, wt, wy, h, deep
        self.te, self.ye = t + 2 * wt, y + 2 * wy
        self.blocks = y // wy

    def units(self, a, b, c):
        if c:
            return (self.wy if b else self.y) // 4
        extra = self.t // 4 if self.deep and b and not a else 0
        return (self.wt if a else self.t) * (self.wy if b else self.y) // 4 + extra

    def scratch(self, tag):
        vmem = lambda *shape: pltpu.VMEM(shape + (128,), F32)
        made = {
            "st": vmem(self.t, self.y), "py": vmem(2, self.t, self.wy), "lt": vmem(self.te, self.y),
            "ly": vmem(2, self.te, self.wy), "pf": vmem(self.blocks, self.wy), "pl": vmem(self.blocks, self.wy),
            "lz": vmem(2, 3, self.blocks, self.wy), "lzb": vmem(2, 3, 2, self.wy)}
        if self.deep:
            made.update(ky=vmem(2, self.t), lk=vmem(2, self.t))
        return {name + tag: value for name, value in made.items()}


NEAR = [(a, b, c) for c in (-1, 0, 1) for b in (-1, 0, 1) for a in (-1, 0, 1) if (a, b, c) != (0, 0, 0)]


def near(offset, counts):
    target, exists = {}, None
    for axis, step in zip(("gx", "gy", "gz"), offset):
        me, n = lax.axis_index(axis), counts[axis]
        if step:
            target[axis] = lax.rem(me + step + n, n)
            inside = me > 0 if step < 0 else me < n - 1
            exists = inside if exists is None else jnp.logical_and(exists, inside)
    return target, exists


def wait_units(units, count, sem):
    part = units.at[pl.ds(0, count)]
    pltpu.make_async_copy(part, part, sem).wait()


def wait_near(lv, counts, units, sems):
    choices = []
    for axis in ("gx", "gy", "gz"):
        me, n = lax.axis_index(axis), counts[axis]
        if n == 1:
            choices.append([(0, None)])
        elif n == 2:
            choices.append([(1, None)])
        else:
            edge = jnp.logical_or(me == 0, me == n - 1)
            choices.append([(1, edge), (2, jnp.logical_not(edge))])
    for chosen in itertools.product(*choices):
        total = 0
        for kind in itertools.product((0, 1), repeat=3):
            if any(kind):
                copies = 1
                for used, (number, _) in zip(kind, chosen):
                    copies *= number if used else 1
                total += copies * lv.units(*kind)
        conditions = [condition for _, condition in chosen if condition is not None]

        def wait():
            for sem in sems:
                wait_units(units, total, sem)

        if conditions:
            pl.when(functools.reduce(jnp.logical_and, conditions))(wait)
        else:
            wait()


def clear_sides(lv, b):
    b["lt"][0 : lv.wt] = jnp.zeros((lv.wt, lv.y, 128), F32)
    b["lt"][lv.t + lv.wt : lv.te] = jnp.zeros((lv.wt, lv.y, 128), F32)
    for name in ("ly", "lz", "lzb") + (("lk",) if lv.deep else ()):
        b[name][...] = jnp.zeros(b[name].shape, F32)


def pack_sides(lv, b):
    h, st, lane = lv.h, b["st"], iota((lv.y, 128), 1)
    if lv.blocks > 1:
        b["py"][0] = st[:, 0 : lv.wy, :]
        b["py"][1] = st[:, lv.y - lv.wy : lv.y, :]
    first = last = jnp.zeros((lv.y, 128), F32)
    for t in range(lv.t):
        tile = st[t]
        for half in range(2):
            at = 2 * h * t + h * half
            turned = pltpu.roll(tile, (at - 64 * half) % 128, 1)
            first = jnp.where(((lane - at) & 127) < h, turned, first)
            last = jnp.where(((lane - at - 64 + h) & 127) < h, turned, last)
        if lv.deep:
            b["ky"][0, t : t + 1, :] = tile[lv.wy : lv.wy + 1, :]
            b["ky"][1, t : t + 1, :] = tile[lv.y - lv.wy - 1 : lv.y - lv.wy, :]
    for block in range(lv.blocks):
        rows = slice(block * lv.wy, block * lv.wy + lv.wy)
        b["pf"][block], b["pl"][block] = first[rows], last[rows]


def send_sides(lv, b, sems, counts):
    taken = {-1: (0, lv.wt), 0: (0, lv.t), 1: (lv.t - lv.wt, lv.wt)}
    landed = {-1: lv.t + lv.wt, 0: lv.wt, 1: 0}
    for x, y, z in reversed(sorted(NEAR, key=lambda n: (n[0] != 0) + (n[1] != 0) + (n[2] != 0))):
        target, exists = near((x, y, z), counts)
        first, count = taken[x]
        source, goal, side = pl.ds(first, count), pl.ds(landed[x], count), (y + 1) // 2
        if z:
            ends = b["pf"] if z < 0 else b["pl"]
            if y:
                pairs = [(ends.at[0 if y < 0 else lv.blocks - 1], b["lzb"].at[(1 - z) // 2, 1 - x, (1 - y) // 2])]
            else:
                pairs = [(ends, b["lz"].at[(1 - z) // 2, 1 - x])]
        elif y:
            pairs = [(b["py"].at[side, source] if lv.blocks > 1 else b["st"].at[source], b["ly"].at[side, goal])]
            if lv.deep and not x:
                pairs.append((b["ky"].at[side], b["lk"].at[side]))
        else:
            pairs = [(b["st"].at[source], b["lt"].at[goal])]
        for src, dst in pairs:
            copy = pltpu.make_async_remote_copy(
                src, dst, sems.at[0], sems.at[1], device_id=target, device_id_type=MESH)
            pl.when(exists)(copy.start)


def take_sides(lv, b, sems, counts, units, emit):
    h, wt = lv.h, lv.wt
    wait_near(lv, counts, units, (sems.at[0], sems.at[1]))
    lane = iota((lv.ye, 128), 1)
    own, edge = lane < 64, (lane < 64 + h) | (lane >= 128 - h)
    for a in range(3):
        low, high = [
            jnp.concatenate(
                [b["lz"][c, a, block] for block in range(lv.blocks)] + [b["lzb"][c, a, 1], b["lzb"][c, a, 0]], axis=0)
            for c in range(2)]
        mixed = [jnp.where(((lane - 16 * h * q + h) & 127) < 64, high, low) for q in range(-(-lv.t // 8))]
        place = (0, wt, lv.t + wt)[a]
        start, count = ((lv.t - wt, wt), (0, lv.t), (0, wt))[a]
        for k in range(count):
            n, t = start + k, place + k
            rows = b["st"][n] if a == 1 else b["lt"][t]
            full = jnp.concatenate([rows, b["ly"][0, t], b["ly"][1, t]], axis=0)
            slices = []
            for half in range(2):
                ends = pltpu.roll(mixed[n // 8], (64 - 2 * h * n - h * half) % 128, 1)
                values = pltpu.roll(full, 64, 1) if half else full
                slices.append(jnp.where(own, values, jnp.where(edge, ends, 0.0)))
            emit(t, *slices)


def gather_start(buf, sems, counts):
    me = {axis: lax.axis_index(axis) for axis in counts}
    mine = buf.at[me["gx"], me["gy"], me["gz"]]
    ranges = [[n - k if k else 0 for k in range(n)] for n in counts.values()]
    for offset in sorted(itertools.product(*ranges), key=lambda o: -sum(1 for k in o if k)):
        if any(offset):
            target = {axis: lax.rem(me[axis] + k, counts[axis]) for axis, k in zip(counts, offset) if k}
            pltpu.make_async_remote_copy(
                mine, mine, sems.at[0], sems.at[1], device_id=target, device_id_type=MESH).start()


def gather_wait(sems, counts, units):
    others = counts["gx"] * counts["gy"] * counts["gz"] - 1
    if others:
        wait_units(units, others, sems.at[0])
        wait_units(units, others, sems.at[1])


def batches(low, high, size, body):
    whole = (high - low) // size
    if whole:
        def run(step, carry):
            body(low + step * size, size)
            return carry

        lax.fori_loop(0, whole, run, 0)
    if low + whole * size < high:
        body(low + whole * size, high - low - whole * size)


def even_rows(x, rows):
    return ((iota((rows, 128), 0) + x) & 1) == 0


def prepare_fine(lv, k, rows, fx, fy, zs, zo, dd, iv):
    row = iota((lv.ye, 128), 0)

    def body(first, count, inside=False):
        made = []
        for x in [first + i for i in range(count)]:
            first_red = even_rows(x, lv.ye)
            mids = [k[c][x + 1] for c in range(2)]
            for c in range(2):
                kx, other = mids[c], mids[1 - c]
                below = 0.5 * (k[1 - c][x] + kx)
                above = 0.5 * (kx + k[1 - c][x + 2])
                lower, upper = up(other, 0), down(other, 0)
                if inside:
                    ends = [jnp.broadcast_to(rows[side, pl.ds(x - lv.wt, 1), :], (lv.ye, 128)) for side in range(2)]
                    if c == 0:
                        ends = [pltpu.roll(end, 64, 1) for end in ends]
                    upper = jnp.where(row == lv.y + lv.wy - 1, ends[0], upper)
                    lower = jnp.where(row == lv.y + lv.wy, ends[1], lower)
                second = 0.5 * (lower + kx)
                same = 0.5 * (kx + other)
                moved = [up(other, 1), down(other, 1)]
                third = 0.5 * (kx + jnp.where(first_red, moved[c], moved[1 - c]))
                total = below + above + second + 0.5 * (kx + upper) + same + third
                made.append((x, c, below, second, third, total, jnp.where(kx > 0.0, 1.0 / total, 0.0), same))
        for x, c, *values, same in made:
            for ref, value in zip((fx, fy, zo, dd, iv), values):
                ref[c][x] = value
            if c == 0:
                zs[x] = same

    batches(0, lv.wt, 2, body)
    batches(lv.wt, lv.wt + lv.t, 2, functools.partial(body, inside=True))
    batches(lv.wt + lv.t, lv.te, 2, body)


def around_fine(lv, v, c, x, faces):
    fx, fy, zs, zo = faces
    o = 1 - c
    mid, first_red = v[o][x], even_rows(x, lv.ye)
    moved = [up(mid, 1), down(mid, 1)]
    summed = fx[c][x] * v[o][x - 1] + fx[o][x + 1] * v[o][x + 1]
    summed = summed + fy[c][x] * up(mid, 0) + down(fy[o][x] * mid, 0)
    return summed + zs[x] * mid + zo[c][x] * jnp.where(first_red, moved[c], moved[o])


def half_sweep_fine(lv, v, g, faces, iv, c, reach):
    low, high = lv.wt - reach, lv.wt + lv.t + reach

    def body(first, count):
        fresh = [(x, (g[c][x] + around_fine(lv, v, c, x, faces)) * iv[c][x]) for x in [first + i for i in range(count)]]
        for x, value in fresh:
            v[c][x] = value

    batches(low, high, (high - low) // 2, body)


def residual_fine(lv, v, g, faces, dd, pairs):
    def body(first, count):
        made = []
        for i in [first + j for j in range(count)]:
            total = jnp.zeros((lv.ye, 128), F32)
            for x in (lv.wt + 2 * i, lv.wt + 2 * i + 1):
                for c in range(2):
                    total = total + (g[c][x] - dd[c][x] * v[c][x] + around_fine(lv, v, c, x, faces))
            made.append((i, total))
        for i, total in made:
            pairs[i] = total[0 : lv.y, :]

    batches(0, lv.t // 2, 4, body)


def prepare(k, fx, fy, fz, dd, iv):
    planes = k.shape[0]

    def body(first, count):
        made = []
        for x in [first + i for i in range(count)]:
            kx = k[x]
            below = 0.5 * (k[jnp.maximum(x - 1, 0)] + kx)
            above = 0.5 * (kx + k[jnp.minimum(x + 1, planes - 1)])
            second = 0.5 * (up(kx, 0) + kx)
            third = 0.5 * (up(kx, 1) + kx)
            total = below + above + second + down(second, 0) + third + down(third, 1)
            made.append((x, below, second, third, total, jnp.where(kx > 0.0, 1.0 / total, 0.0)))
        for x, *values in made:
            for ref, value in zip((fx, fy, fz, dd, iv), values):
                ref[x] = value

    batches(0, planes, 4, body)


def around(v, x, mid, faces):
    fx, fy, fz = faces
    second, third = fy[x], fz[x]
    summed = fx[x] * v[x - 1] + fx[x + 1] * v[x + 1]
    summed = summed + second * up(mid, 0) + down(second * mid, 0)
    return summed + third * up(mid, 1) + down(third * mid, 1)


def half_sweep(v, g, faces, iv, colour, low, high):
    parity = iota(v.shape[1:], 0) + iota(v.shape[1:], 1)

    def body(first, count):
        fresh = []
        for x in [first + i for i in range(count)]:
            mid = v[x]
            value = (g[x] + around(v, x, mid, faces)) * iv[x]
            fresh.append((x, jnp.where(((parity + x) & 1) == colour, value, mid)))
        for x, value in fresh:
            v[x] = value

    batches(low, high, 10, body)


def residual_pairs(v, g, faces, dd, pairs, halo):
    for i in range(pairs.shape[0]):
        total = jnp.zeros(v.shape[1:], F32)
        for x in (halo + 2 * i, halo + 2 * i + 1):
            mid = v[x]
            total = total + (g[x] - dd[x] * mid + around(v, x, mid, faces))
        pairs[i] = 0.25 * total[0 : pairs.shape[1]]


def pair_planes(planes, target):
    lane = iota(planes[0].shape, 1)
    for t in range(len(planes) // 2):
        target[t] = jnp.where(lane < 64, planes[2 * t], pltpu.roll(planes[2 * t + 1], 64, 1))


def fold_rows(pairs, rows):
    return pairs[:, pl.ds(0, rows, stride=2), :] + pairs[:, pl.ds(1, rows, stride=2), :]


def dot(a, b):
    return jnp.dot(a, b, precision=HIGH, preferred_element_type=F32)


def split_lanes(transposed):
    cell, lane = iota((128, 128), int(transposed)), iota((128, 128), 1 - int(transposed))
    return jnp.where(lane == cell // 2 + 64 * (cell % 2), 1.0, 0.0).astype(F32)


def coarse_low(pairs, count, rows, lanes, tmp):
    total = jnp.zeros((rows, 128), F32)
    source, goal = iota((128, 128), 0), iota((128, 128), 1)
    for x in range(count):
        matrix = jnp.where((source // 2 + x * lanes == goal) & (source < 2 * lanes), 0.125, 0.0).astype(F32)
        total = total + dot(pairs[x], matrix)
    tmp[...] = total
    half = rows // 2
    return tmp[pl.ds(0, half, stride=2), :] + tmp[pl.ds(1, half, stride=2), :]


def repeat(count, body, carry):
    if count <= 16:
        for p in range(count):
            carry = body(p, carry)
        return carry
    return lax.fori_loop(0, count, body, carry)


def spread_low(buf, whole, counts, pad):
    lane = iota((8, 128), 1)

    def body(a, carry):
        for ct in range(counts["gy"] // 2):
            for gt in range(counts["gz"] // 4):
                pieces = [
                    jnp.concatenate([buf[a, 2 * ct, 4 * gt + g], buf[a, 2 * ct + 1, 4 * gt + g]], axis=0)
                    for g in range(4)]
                for i in range(4):
                    total = pieces[0] if i == 0 else pltpu.roll(pieces[0], (-32 * i) % 128, 1)
                    for g in range(1, 4):
                        piece = pieces[g] if g == i else pltpu.roll(pieces[g], (32 * (g - i)) % 128, 1)
                        total = jnp.where(lane // 32 == g, piece, total)
                    whole[pad + 4 * a + i, 8 * ct : 8 * ct + 8, 128 * gt : 128 * gt + 128] = total
        return carry

    repeat(counts["gx"], body, 0)


def low_faces(k, faces, dims, pad):
    planes, rows, lanes = dims
    cx, cy0, cy1, cz0, cz1, cd = faces
    row, lane = iota((rows, lanes), 0), iota((rows, lanes), 1)
    scale = 0.5 * 0.0625

    def body(p, carry):
        kx = k[p + pad]
        below, above = scale * (k[p + pad - 1] + kx), scale * (kx + k[p + pad + 1])
        total = below + above
        cx[p] = below
        cx[p + 1] = above
        for target, inside, moved in (
            (cy0, row > 0, up(kx, 0)), (cy1, row < rows - 1, down(kx, 0)),
            (cz0, lane > 0, up(kx, 1)), (cz1, lane < lanes - 1, down(kx, 1))):
            face = scale * (kx + moved)
            target[p] = jnp.where(inside, face, 0.0)
            total = total + jnp.where(inside, face, scale * kx)
        cd[p] = total
        return carry

    repeat(planes, body, 0)


def bottom(f, s, vv, faces, dims, pad):
    planes, rows, lanes = dims
    cx, cy0, cy1, cz0, cz1, cd = faces

    def operate(v, p):
        mid = v[p + pad]
        summed = cx[p] * v[p + pad - 1] + cx[p + 1] * v[p + pad + 1]
        summed = summed + (cy0[p] * up(mid, 0) + cy1[p] * down(mid, 0))
        summed = summed + (cz0[p] * up(mid, 1) + cz1[p] * down(mid, 1))
        return mid, cd[p] * mid - summed

    zero = jnp.zeros((rows, lanes), F32)

    def first(p, carry):
        mid, image = operate(f, p)
        vv[p] = image
        return carry[0] + mid * mid, carry[1] + mid * image

    def total(v):
        return jnp.sum(jnp.sum(v, axis=0, keepdims=True), axis=1, keepdims=True)

    norm, along = repeat(planes, first, (zero, zero))
    alpha = total(norm) / total(along)

    def rest(p, carry):
        s[p + pad] = f[p + pad] - alpha * vv[p]
        return carry

    repeat(planes, rest, 0)

    def second(p, carry):
        mid, image = operate(s, p)
        return carry[0] + image * mid, carry[1] + image * image

    turned, norm = repeat(planes, second, (zero, zero))
    return alpha, total(turned) / total(norm)


def pack_boxes(slots, ids, outgoing, boxes, groups):
    held = ids[0].astype(F32)
    cap = held.shape[1]
    eye = iota((cap, cap), 0) == iota((cap, cap), 1)
    rows = jnp.broadcast_to(held, (cap, cap))
    cols = jnp.broadcast_to(jnp.sum(jnp.where(eye, rows, 0.0), axis=1, keepdims=True), (cap, cap))

    def target(v):
        return jnp.floor((v + 0.5) * (1.0 / boxes))

    earlier = (target(rows) == target(cols)) & (cols < rows) & (cols >= 0.0)
    ranking = jnp.sum(jnp.where(earlier, 1.0, 0.0), axis=0, keepdims=True)
    send_row = jnp.where(held >= 0.0, target(held) * SEND + ranking, -1.0)
    count = groups * SEND
    picker = jnp.where(iota((count, cap), 0).astype(F32) == jnp.broadcast_to(send_row, (count, cap)), 1.0, 0.0)
    data = slots[0, 0].astype(F32)
    total = jnp.zeros((count, data.shape[1]), F32)
    for q in range(cap):
        total = total + picker[:, q : q + 1] * data[q : q + 1, :]
    for t in range(groups):
        outgoing[t] = total[SEND * t : SEND * t + SEND, :].astype(BF16)


def place_boxes(incoming, held, owner, lhs, rhs, boxes, groups):
    me = lax.axis_index("gz")
    owners = jnp.broadcast_to(owner[0].astype(F32), (boxes, owner.shape[2]))
    here = iota(owners.shape, 1) == iota(owners.shape, 0) + me * boxes
    col = jnp.sum(jnp.where(here, owners, 0.0), axis=1, keepdims=True)
    cols = jnp.broadcast_to(col, (boxes, boxes))
    first, second = iota((boxes, boxes), 0), iota((boxes, boxes), 1)
    row = jnp.sum(jnp.where(first == second, cols, 0.0), axis=0, keepdims=True)
    before = (jnp.broadcast_to(row, (boxes, boxes)) == cols) & (second < first)
    pick = col * SEND + jnp.sum(jnp.where(before, 1.0, 0.0), axis=1, keepdims=True)
    for t in range(groups):
        held[SEND * t : SEND * t + SEND, :] = incoming[t].astype(F32)
    face = BOX * BOX
    mine = iota((BOX, face), 1) // BOX == iota((BOX, face), 0)
    for i in range(BOX):
        chosen = jnp.zeros((boxes, face), F32)
        for r in range(groups * SEND):
            chosen = jnp.where(pick == float(r), held[r : r + 1, face * i : face * i + face], chosen)
        for b in range(boxes):
            piece = jnp.where(mine, jnp.broadcast_to(chosen[b : b + 1, :], (BOX, face)), 0.0)
            lhs[BOX * i : BOX * i + BOX, face * b : face * b + face] = piece.astype(BF16)
    return jnp.dot(lhs[...], rhs[...], preferred_element_type=F32)


def kernel(levels, counts, names, slots_in, ids_in, owner_in, coef_in, out, *scratch):
    r = dict(zip(names, scratch))
    groups = counts["gz"]
    at = {axis: lax.axis_index(axis) for axis in counts}
    slots, ids, owner, coef, units = r["slots"], r["ids"], r["owner"], r["coef"], r["units"]
    loads = [
        pltpu.make_async_copy(source, target, r["loads"].at[n])
        for n, (source, target) in enumerate(((slots_in, slots), (ids_in, ids), (coef_in, coef), (owner_in, owner)))]
    for load in loads:
        load.start()
    fine, mid = levels["f"], levels["g"]
    sides = {tag: {name[: -len(tag)]: r[name] for name in lv.scratch(tag)} for tag, lv in levels.items()}
    for tag, lv in levels.items():
        clear_sides(lv, sides[tag])

    barrier = pltpu.get_barrier_semaphore()
    expected = 0
    for offset in NEAR:
        target, exists = near(offset, counts)

        @pl.when(exists)
        def _():
            pl.semaphore_signal(barrier, inc=1, device_id=target, device_id_type=MESH)

        expected = expected + jnp.where(exists, 1, 0)
    others = [{"gz": lax.rem(at["gz"] + k, groups)} for k in range(1, groups)]
    if counts["gx"] > 4 or counts["gy"] > 4:
        for offset in itertools.product(*[range(n) for n in counts.values()]):
            if any(offset):
                others.append({axis: lax.rem(at[axis] + k, counts[axis]) for axis, k in zip(counts, offset) if k})
    for target in others:
        pl.semaphore_signal(barrier, inc=1, device_id=target, device_id_type=MESH)

    sems = {tag: r["sems"].at[n] for n, tag in enumerate(("k", "c", "f", "g", "q", "e", "move", "low_k", "low_f"))}

    def send(tag):
        send_sides(levels[tag], sides[tag], sems[tag], counts)

    def take(tag, emit):
        take_sides(levels[tag], sides[tag], sems[tag], counts, units, emit)

    loads[0].wait()
    loads[1].wait()
    boxes = r["boxes"].shape[0] // BOX
    pack_boxes(slots, ids, r["outgoing"], boxes, groups)
    loads[2].wait()
    swap = lambda tile, t: jnp.where(even_rows(t, fine.y), tile, pltpu.roll(tile, 64, 1))
    split = dot(coef[...].reshape(fine.t * fine.y, 128), split_lanes(False)).reshape(fine.t, fine.y, 128)
    for t in range(fine.t):
        sides["k"]["st"][t] = swap(split[t], t)
    pack_sides(levels["k"], sides["k"])
    pl.semaphore_wait(barrier, expected + len(others))

    me = at["gz"]
    for k in range(1, groups):
        to = lax.rem(me + k, groups)
        pltpu.make_async_remote_copy(
            r["outgoing"].at[to], r["incoming"].at[me], sems["move"].at[0], sems["move"].at[1],
            device_id={"gz": to}, device_id_type=MESH).start()
    send("k")
    r["incoming"][me] = r["outgoing"][me]

    half_t, half_y = fine.t // 2, fine.y // 2
    for i in range(half_t):
        pair = sides["k"]["st"][2 * i] + sides["k"]["st"][2 * i + 1]
        r["pairs"][i] = pair + pltpu.roll(pair, 64, 1)
    coarse = 0.125 * fold_rows(r["pairs"], half_y)
    pair_planes([coarse[i] for i in range(half_t)], sides["c"]["st"])
    pack_sides(mid, sides["c"])
    send("c")
    for i in range(half_t // 2):
        r["pairsm"][i] = coarse[2 * i] + coarse[2 * i + 1]
    here = (at["gx"], at["gy"], at["gz"])
    r["gk"][here] = coarse_low(r["pairsm"], half_t // 2, half_y, 32, r["tmp"])
    lane = iota((BOX * BOX, 128), 1)
    cell = 2 * (lane % 64) + lane // 64
    folded = iota((BOX * BOX, 128), 0) % BOX == cell % BOX
    for b in range(boxes):
        block = jnp.where(folded & (cell // BOX == b), 1.0, 0.0)
        r["rhs"][BOX * BOX * b : BOX * BOX * (b + 1), :] = block.astype(BF16)
    loads[3].wait()
    if groups > 1:
        part = r["incoming"].at[pl.ds(0, groups - 1)]
        for n in range(2):
            pltpu.make_async_copy(part, part, sems["move"].at[n]).wait()
    source = place_boxes(r["incoming"], r["held"], owner, r["lhs"], r["rhs"], boxes, groups)
    source = source.reshape(fine.t, fine.y, 128)
    for t in range(fine.t):
        sides["f"]["st"][t] = swap(source[t], t)
    pack_sides(fine, sides["f"])
    send("f")

    pair_of = lambda name: (r[name + "r"], r[name + "b"])
    v0, g0, k0 = pair_of("v0"), pair_of("g0"), pair_of("k0")
    fx, fy, zo, dd0, iv0 = (pair_of(name) for name in ("fx0", "fy0", "zo0", "dd0", "iv0"))
    faces0 = (fx, fy, r["zs0"], zo)
    faces1 = (r["fx1"], r["fy1"], r["fz1"])
    dd1, iv1, v1, K1, G1, E1 = (r[name] for name in ("dd1", "iv1", "v1", "K1", "G1", "E1"))

    def store_pair(refs):
        def emit(t, first, second):
            refs[0][t] = first
            refs[1][t] = second
        return emit

    def store_planes(ref):
        def emit(t, first, second):
            ref[2 * t] = first
            ref[2 * t + 1] = second
        return emit

    take("k", store_pair(k0))
    prepare_fine(fine, k0, sides["k"]["lk"], fx, fy, r["zs0"], zo, dd0, iv0)
    take("c", store_planes(K1))
    prepare(K1, *faces1, dd1, iv1)
    for name in ("k2", "f2", "s2"):
        r[name][...] = jnp.zeros(r[name].shape, F32)

    def open_fine(t, red, black):
        g0[0][t] = red
        g0[1][t] = black
        v0[0][t] = red * iv0[0][t]

    take("f", open_fine)
    for reach, colour in ((3, 1), (2, 0), (1, 1)):
        half_sweep_fine(fine, v0, g0, faces0, iv0, colour, reach)
    residual_fine(fine, v0, g0, faces0, dd0, r["pairs"])

    coarse = 0.5 * fold_rows(r["pairs"], half_y)
    pair_planes([coarse[i] for i in range(half_t)], sides["g"]["st"])
    pack_sides(mid, sides["g"])
    send("g")
    pair_planes([v0[1][fine.wt + x, 0 : fine.y, :] for x in range(fine.t)], sides["q"]["st"])
    pack_sides(levels["q"], sides["q"])
    send("q")
    wm = 2 * mid.wt
    parity = iota((mid.ye, 128), 0) + iota((mid.ye, 128), 1)

    def open_mid(t, *planes):
        for k, plane in enumerate(planes):
            x = 2 * t + k
            G1[x] = plane
            v1[x] = jnp.where(((parity + x) & 1) == 0, plane * iv1[x], 0.0)

    take("g", open_mid)
    gather_start(r["gk"], sems["low_k"], counts)
    for reach, colour in ((3, 1), (2, 0), (1, 1)):
        half_sweep(v1, G1, faces1, iv1, colour, wm - reach, wm + half_t + reach)
    pair_planes([v1[wm + x, 0 : mid.y, :] for x in range(half_t)], sides["e"]["st"])
    pack_sides(mid, sides["e"])
    send("e")
    residual_pairs(v1, G1, faces1, dd1, r["pairsm"], wm)
    r["gf"][here] = coarse_low(r["pairsm"], half_t // 2, half_y, 32, r["tmp"])
    gather_start(r["gf"], sems["low_f"], counts)

    planes, rows, lanes = dims = (4 * counts["gx"], 4 * counts["gy"], 32 * counts["gz"])
    pad = wm // 2
    low = tuple(r[name] for name in ("cx", "cy0", "cy1", "cz0", "cz1", "cd"))
    take("q", store_planes(r["q0"]))
    gather_wait(sems["low_k"], counts, units)
    spread_low(r["gk"], r["k2"], counts, pad)
    low_faces(r["k2"], low, dims, pad)
    take("e", store_planes(E1))
    gather_wait(sems["low_f"], counts, units)
    spread_low(r["gf"], r["f2"], counts, pad)
    alpha, omega = bottom(r["f2"], r["s2"], r["v2"], low, dims, pad)
    around_low = mid.te
    for q in range(around_low):
        turned = alpha * r["f2"][4 * at["gx"] + q] + omega * r["s2"][4 * at["gx"] + q]
        plane = turned
        for c in range(1, counts["gy"]):
            turned = jnp.where(at["gy"] == c, pltpu.roll(plane, rows - 4 * c, 0), turned)
        r["local"][q, 0:8, :] = turned[0:8, :]
        r["local"][q, 8:16, :] = pltpu.roll(turned[rows - 8 : rows, :], 4, 0)
    goal = iota((lanes, 128), 1)
    cell = jnp.where(goal < 64 + wm, goal, goal - 128)
    cell = (cell + 128) // 2 - 64
    wanted = (goal < 64 + wm) | (goal >= 128 - wm)
    matrix = jnp.where((iota((lanes, 128), 0) == 32 * at["gz"] + cell) & wanted, 1.0, 0.0).astype(F32)
    spread = dot(r["local"][...].reshape(16 * around_low, lanes), matrix).reshape(around_low, 16, 128)
    for q in range(around_low):
        wide = r["wide"].at[q]
        for k in range(2):
            wide[pl.ds(k, 12, stride=2), :] = spread[q, 0:12]
        for k in range(2):
            x = 2 * q + k
            E1[x] = jnp.where(K1[x] > 0.0, E1[x] + wide[...], 0.0)
    for reach, colour in ((5, 0), (4, 1), (3, 0), (2, 1)):
        half_sweep(E1, G1, faces1, iv1, colour, wm - reach, wm + half_t + reach)

    low_w = fine.wt // 2
    row = iota((8, 128), 0)
    for i in range(half_t + 2 * low_w):
        x = wm - low_w + i
        wide = r["wide"].at[i]
        ends = jnp.where(row < low_w, E1[x, 8:16, :], pltpu.roll(E1[x, mid.ye - 8 : mid.ye, :], 4, 0))
        turned = jnp.concatenate([E1[x, 0:8, :], ends[0:4]], axis=0)
        for k in range(2):
            wide[pl.ds(k, 12, stride=2), :] = turned
        for k in range(2):
            v0[1][2 * i + k] = r["q0"][2 * i + k] + wide[...]
    for reach, colour in ((3, 0), (2, 1), (1, 0), (0, 1)):
        half_sweep_fine(fine, v0, g0, faces0, iv0, colour, reach)
    lane = iota((fine.y, 128), 1)
    for t in range(fine.t):
        red, black = (v0[c][fine.wt + t, 0 : fine.y, :] for c in range(2))
        r["joined"][t] = swap(jnp.where(lane < 64, red, pltpu.roll(black, 64, 1)), t)
    joined = dot(r["joined"][...].reshape(fine.t * fine.y, 128), split_lanes(True))
    out[...] = joined.reshape(out.shape)


def per_device(counts, old_slots, old_ids, old_owner, coefficient):
    x, y, z = coefficient.shape
    planes, rows, lanes = 4 * counts["gx"], 4 * counts["gy"], 32 * counts["gz"]
    groups, boxes = counts["gz"], z // BOX
    cells = old_slots.shape[3]
    mid = Level(x // 4, y // 2, 3, 8, 6)
    levels = {
        "k": Level(x, y, 5, 4, 3, deep=True), "f": Level(x, y, 4, 4, 2), "q": Level(x // 2, y, 2, 4, 2),
        "c": mid, "g": mid, "e": mid}
    fine, edge = levels["f"], levels["k"]
    pad = mid.wt
    devices = counts["gx"] * counts["gy"] * groups
    vmem = lambda *shape: pltpu.VMEM(shape, F32)
    dma = lambda *shape: pltpu.SemaphoreType.DMA(shape)
    scratch = {}
    for tag, level in levels.items():
        scratch.update(level.scratch(tag))
    for name in ("v0", "g0", "fx0", "fy0", "zo0", "dd0", "iv0", "k0"):
        for colour in "rb":
            scratch[name + colour] = vmem(edge.te if name == "k0" else fine.te, fine.ye, 128)
    for name in ("zs0", "q0"):
        scratch[name] = vmem(fine.te, fine.ye, 128)
    for name in ("fx1", "fy1", "fz1", "dd1", "iv1", "v1", "K1", "G1", "E1"):
        scratch[name] = vmem(2 * mid.te, mid.ye, 128)
    scratch.update(
        slots=pltpu.VMEM(old_slots.shape, old_slots.dtype), ids=pltpu.VMEM(old_ids.shape, old_ids.dtype),
        owner=pltpu.VMEM(old_owner.shape, old_owner.dtype), coef=vmem(*coefficient.shape), loads=dma(4),
        outgoing=pltpu.VMEM((groups, SEND, cells), BF16), incoming=pltpu.VMEM((groups, SEND, cells), BF16),
        held=vmem(groups * SEND, cells), sems=dma(9, 2), units=vmem(max(160, devices), 4, 128),
        lhs=pltpu.VMEM((BOX * BOX, boxes * BOX * BOX), BF16), rhs=pltpu.VMEM((boxes * BOX * BOX, 128), BF16),
        boxes=vmem(boxes * BOX, 128), pairs=vmem(x // 2, y, 128), pairsm=vmem(x // 4, y // 2, 128),
        joined=vmem(x, y, 128), tmp=vmem(y // 2, 128), local=vmem(mid.te, 16, lanes),
        wide=vmem(max(mid.te, fine.te // 2), 24, 128),
        gk=vmem(counts["gx"], counts["gy"], groups, 4, 128), gf=vmem(counts["gx"], counts["gy"], groups, 4, 128),
        cx=vmem(planes + 1, rows, lanes), v2=vmem(planes, rows, lanes))
    for name in ("cy0", "cy1", "cz0", "cz1", "cd"):
        scratch[name] = vmem(planes, rows, lanes)
    for name in ("f2", "k2", "s2"):
        scratch[name] = vmem(planes + 2 * pad, rows, lanes)
    return pl.pallas_call(
        functools.partial(kernel, levels, counts, tuple(scratch)),
        out_shape=jax.ShapeDtypeStruct(coefficient.shape, F32),
        in_specs=[pl.BlockSpec(memory_space=pltpu.MemorySpace.HBM)] * 4,
        out_specs=pl.BlockSpec(memory_space=pltpu.VMEM),
        scratch_shapes=list(scratch.values()),
        compiler_params=pltpu.CompilerParams(
            collective_id=0, has_side_effects=True, vmem_limit_bytes=44 * 1024 * 1024),
    )(*[pltpu.with_memory_space_constraint(v, pltpu.HBM) for v in (old_slots, old_ids, old_owner, coefficient)])


def solution(mesh):
    counts = {axis: mesh.shape[axis] for axis in ("gx", "gy", "gz")}
    return jax.shard_map(
        functools.partial(per_device, counts), mesh=mesh,
        in_specs=(P("gx", "gy", "gz", None), P("gx", "gy", "gz"), P("gx", "gy", None), P("gx", "gy", "gz")),
        out_specs=P("gx", "gy", "gz"), check_vma=False)
```

time: 33 us -> 28.3 us (0.86)
  Pallas kernels: 32.2 us -> 27.5 us
    pallas_call x1, Pallas kernels: 32.2 us -> 27.5 us  [per_device(): pl.pallas_call(functools.partial(kernel, levels, counts, tuple(scratch)),...]
where the time goes in v3:
time: 28.3 us; the launch traced here: 28.1 us
  Pallas kernels  27.5 us (97%)
  local copies, waits for them, and re-layouts  0.66 us (2%)
    pallas_call x1, Pallas kernels, per_device(): pl.pallas_call(functools.partial(kernel, levels, counts, tuple(scratch)),...  27.5 us
    unnamed x1, local copies, waits for them, and re-layouts  0.66 us

profile of v3, /device:TPU:0, one launch (start us, length us, event | category | flops | bytes accessed | tf_op | source)
XLA Modules:
  0.0 28.1 jit_solution(9665445274325111055)
XLA Ops:
  0.0 27.5 %shard_map.46 = f32[16,16,128]{2,1,0:T(8,128)S(1)} custom-call(bf16[1,1,8,4096]{3,2,1,0:T(8,128)(2,1)} %slots_in.1, s32[1,1,8]{2,1,0:T(1,128)} %ids_in.1, s32[1,1,32]{2,1,0:T(1,128)} %owner_in.1, f32[16,16,128]{2,1,0:T(8,128)} %coef_in.1), custom_call_target="tpu_custom_call" | custom-call | tf_op jit(solution)/shard_map/pallas_call | solution.py:757
  27.5 0.7 %copy.6 = f32[16,16,128]{2,1,0:T(8,128)} copy(f32[16,16,128]{2,1,0:T(8,128)S(1)} %shard_map.46) | data formatting | bytes 262144

commit v4 on v3

--- a/solution.py
+++ b/solution.py
@@ -185,7 +185,9 @@
     ranges = [[n - k if k else 0 for k in range(n)] for n in counts.values()]
     for offset in sorted(itertools.product(*ranges), key=lambda o: -sum(1 for k in o if k)):
         if any(offset):
-            target = {axis: lax.rem(me[axis] + k, counts[axis]) for axis, k in zip(counts, offset) if k}
+            target = {
+                axis: lax.rem(me[axis] + jnp.where(me[axis] < counts[axis] // 2, k, counts[axis] - k), counts[axis])
+                for axis, k in zip(counts, offset) if k}
             pltpu.make_async_remote_copy(
                 mine, mine, sems.at[0], sems.at[1], device_id=target, device_id_type=MESH).start()
 
@@ -199,7 +201,9 @@
 
 def batches(low, high, size, body):
     whole = (high - low) // size
-    if whole:
+    if whole == 1:
+        body(low, size)
+    elif whole:
         def run(step, carry):
             body(low + step * size, size)
             return carry
@@ -267,7 +271,7 @@
         for x, value in fresh:
             v[c][x] = value
 
-    batches(low, high, (high - low) // 2, body)
+    batches(low, high, high - low, body)
 
 
 def residual_fine(lv, v, g, faces, dd, pairs):
@@ -282,7 +286,7 @@
         for i, total in made:
             pairs[i] = total[0 : lv.y, :]
 
-    batches(0, lv.t // 2, 4, body)
+    batches(0, lv.t // 2, lv.t // 2, body)
 
 
 def prepare(k, fx, fy, fz, dd, iv):
@@ -325,7 +329,7 @@
         for x, value in fresh:
             v[x] = value
 
-    batches(low, high, 10, body)
+    batches(low, high, high - low, body)
 
 
 def residual_pairs(v, g, faces, dd, pairs, halo):
@@ -351,20 +355,31 @@
     return jnp.dot(a, b, precision=HIGH, preferred_element_type=F32)
 
 
+def pick(values, matrix):
+    parts, rest = [], values
+    for _ in range(3):
+        parts.append(rest.astype(BF16))
+        rest = rest - parts[-1].astype(F32)
+    return jnp.dot(
+        jnp.concatenate(parts, axis=1), jnp.concatenate([matrix.astype(BF16)] * 3, axis=0), preferred_element_type=F32)
+
+
 def split_lanes(transposed):
     cell, lane = iota((128, 128), int(transposed)), iota((128, 128), 1 - int(transposed))
     return jnp.where(lane == cell // 2 + 64 * (cell % 2), 1.0, 0.0).astype(F32)
 
 
-def coarse_low(pairs, count, rows, lanes, tmp):
-    total = jnp.zeros((rows, 128), F32)
+def coarse_low(pairs, tmp):
+    count, rows, _ = pairs.shape
+    half = rows // 2
+    for x in range(count):
+        tmp[half * x : half * x + half, :] = pairs[x, pl.ds(0, half, stride=2), :] + pairs[x, pl.ds(1, half, stride=2), :]
     source, goal = iota((128, 128), 0), iota((128, 128), 1)
-    for x in range(count):
-        matrix = jnp.where((source // 2 + x * lanes == goal) & (source < 2 * lanes), 0.125, 0.0).astype(F32)
-        total = total + dot(pairs[x], matrix)
-    tmp[...] = total
-    half = rows // 2
-    return tmp[pl.ds(0, half, stride=2), :] + tmp[pl.ds(1, half, stride=2), :]
+    means = 0.125 * pick(tmp[...], jnp.where((source // 2 == goal) & (source < 64), 1.0, 0.0))
+    total = means[0:half]
+    for x in range(1, count):
+        total = total + pltpu.roll(means[half * x : half * x + half], 32 * x, 1)
+    return total
 
 
 def repeat(count, body, carry):
@@ -480,7 +495,7 @@
         outgoing[t] = total[SEND * t : SEND * t + SEND, :].astype(BF16)
 
 
-def place_boxes(incoming, held, owner, lhs, rhs, boxes, groups):
+def place_boxes(incoming, held, owner, rows, boxes, groups):
     me = lax.axis_index("gz")
     owners = jnp.broadcast_to(owner[0].astype(F32), (boxes, owner.shape[2]))
     here = iota(owners.shape, 1) == iota(owners.shape, 0) + me * boxes
@@ -492,16 +507,19 @@
     pick = col * SEND + jnp.sum(jnp.where(before, 1.0, 0.0), axis=1, keepdims=True)
     for t in range(groups):
         held[SEND * t : SEND * t + SEND, :] = incoming[t].astype(F32)
-    face = BOX * BOX
-    mine = iota((BOX, face), 1) // BOX == iota((BOX, face), 0)
-    for i in range(BOX):
-        chosen = jnp.zeros((boxes, face), F32)
+    per = 128 // BOX
+    lane_box, row = iota((boxes, 128), 1) // BOX, iota((boxes, 128), 0)
+    for part in range(BOX * BOX // per):
+        lanes = slice(128 * part, 128 * part + 128)
+        chosen = jnp.zeros((boxes, 128), F32)
         for r in range(groups * SEND):
-            chosen = jnp.where(pick == float(r), held[r : r + 1, face * i : face * i + face], chosen)
-        for b in range(boxes):
-            piece = jnp.where(mine, jnp.broadcast_to(chosen[b : b + 1, :], (BOX, face)), 0.0)
-            lhs[BOX * i : BOX * i + BOX, face * b : face * b + face] = piece.astype(BF16)
-    return jnp.dot(lhs[...], rhs[...], preferred_element_type=F32)
+            chosen = jnp.where(pick == float(r), held[r : r + 1, lanes], chosen)
+        total = chosen
+        for d in range(1, boxes):
+            moved = pltpu.roll(pltpu.roll(chosen, BOX * d, 1), boxes - d, 0)
+            total = jnp.where(((lane_box - row) & (boxes - 1)) == d, moved, total)
+        rows[per * part : per * part + per, :] = total
+    return jnp.dot(rows[...].astype(BF16), split_lanes(False).astype(BF16), preferred_element_type=F32)
 
 
 def kernel(levels, counts, names, slots_in, ids_in, owner_in, coef_in, out, *scratch):
@@ -521,7 +539,7 @@
 
     barrier = pltpu.get_barrier_semaphore()
     expected = 0
-    for offset in NEAR:
+    for offset in sorted(NEAR, key=lambda n: -sum(map(abs, n))):
         target, exists = near(offset, counts)
 
         @pl.when(exists)
@@ -547,14 +565,8 @@
 
     loads[0].wait()
     loads[1].wait()
-    boxes = r["boxes"].shape[0] // BOX
+    boxes = out.shape[2] // BOX
     pack_boxes(slots, ids, r["outgoing"], boxes, groups)
-    loads[2].wait()
-    swap = lambda tile, t: jnp.where(even_rows(t, fine.y), tile, pltpu.roll(tile, 64, 1))
-    split = dot(coef[...].reshape(fine.t * fine.y, 128), split_lanes(False)).reshape(fine.t, fine.y, 128)
-    for t in range(fine.t):
-        sides["k"]["st"][t] = swap(split[t], t)
-    pack_sides(levels["k"], sides["k"])
     pl.semaphore_wait(barrier, expected + len(others))
 
     me = at["gz"]
@@ -563,6 +575,22 @@
         pltpu.make_async_remote_copy(
             r["outgoing"].at[to], r["incoming"].at[me], sems["move"].at[0], sems["move"].at[1],
             device_id={"gz": to}, device_id_type=MESH).start()
+    greeted = 0
+    for offset in itertools.product((-1, 1), (0,), (-1, 0, 1)):
+        target, exists = near(offset, counts)
+
+        @pl.when(exists)
+        def _():
+            pl.semaphore_signal(r["hello"], inc=1, device_id=target, device_id_type=MESH)
+
+        greeted = greeted + jnp.where(exists, 1, 0)
+
+    loads[2].wait()
+    swap = lambda tile, t: jnp.where(even_rows(t, fine.y), tile, pltpu.roll(tile, 64, 1))
+    split = pick(coef[...].reshape(fine.t * fine.y, 128), split_lanes(False)).reshape(fine.t, fine.y, 128)
+    for t in range(fine.t):
+        sides["k"]["st"][t] = swap(split[t], t)
+    pack_sides(levels["k"], sides["k"])
     send("k")
     r["incoming"][me] = r["outgoing"][me]
 
@@ -577,23 +605,18 @@
     for i in range(half_t // 2):
         r["pairsm"][i] = coarse[2 * i] + coarse[2 * i + 1]
     here = (at["gx"], at["gy"], at["gz"])
-    r["gk"][here] = coarse_low(r["pairsm"], half_t // 2, half_y, 32, r["tmp"])
-    lane = iota((BOX * BOX, 128), 1)
-    cell = 2 * (lane % 64) + lane // 64
-    folded = iota((BOX * BOX, 128), 0) % BOX == cell % BOX
-    for b in range(boxes):
-        block = jnp.where(folded & (cell // BOX == b), 1.0, 0.0)
-        r["rhs"][BOX * BOX * b : BOX * BOX * (b + 1), :] = block.astype(BF16)
+    r["gk"][here] = coarse_low(r["pairsm"], r["tmp"])
     loads[3].wait()
     if groups > 1:
         part = r["incoming"].at[pl.ds(0, groups - 1)]
         for n in range(2):
             pltpu.make_async_copy(part, part, sems["move"].at[n]).wait()
-    source = place_boxes(r["incoming"], r["held"], owner, r["lhs"], r["rhs"], boxes, groups)
+    source = place_boxes(r["incoming"], r["held"], owner, r["rows"], boxes, groups)
     source = source.reshape(fine.t, fine.y, 128)
     for t in range(fine.t):
         sides["f"]["st"][t] = swap(source[t], t)
     pack_sides(fine, sides["f"])
+    pl.semaphore_wait(r["hello"], greeted)
     send("f")
 
     pair_of = lambda name: (r[name + "r"], r[name + "b"])
@@ -617,10 +640,6 @@
 
     take("k", store_pair(k0))
     prepare_fine(fine, k0, sides["k"]["lk"], fx, fy, r["zs0"], zo, dd0, iv0)
-    take("c", store_planes(K1))
-    prepare(K1, *faces1, dd1, iv1)
-    for name in ("k2", "f2", "s2"):
-        r[name][...] = jnp.zeros(r[name].shape, F32)
 
     def open_fine(t, red, black):
         g0[0][t] = red
@@ -639,6 +658,11 @@
     pair_planes([v0[1][fine.wt + x, 0 : fine.y, :] for x in range(fine.t)], sides["q"]["st"])
     pack_sides(levels["q"], sides["q"])
     send("q")
+    gather_start(r["gk"], sems["low_k"], counts)
+    take("c", store_planes(K1))
+    prepare(K1, *faces1, dd1, iv1)
+    for name in ("k2", "f2", "s2"):
+        r[name][...] = jnp.zeros(r[name].shape, F32)
     wm = 2 * mid.wt
     parity = iota((mid.ye, 128), 0) + iota((mid.ye, 128), 1)
 
@@ -649,15 +673,14 @@
             v1[x] = jnp.where(((parity + x) & 1) == 0, plane * iv1[x], 0.0)
 
     take("g", open_mid)
-    gather_start(r["gk"], sems["low_k"], counts)
     for reach, colour in ((3, 1), (2, 0), (1, 1)):
         half_sweep(v1, G1, faces1, iv1, colour, wm - reach, wm + half_t + reach)
+    residual_pairs(v1, G1, faces1, dd1, r["pairsm"], wm)
+    r["gf"][here] = coarse_low(r["pairsm"], r["tmp"])
+    gather_start(r["gf"], sems["low_f"], counts)
     pair_planes([v1[wm + x, 0 : mid.y, :] for x in range(half_t)], sides["e"]["st"])
     pack_sides(mid, sides["e"])
     send("e")
-    residual_pairs(v1, G1, faces1, dd1, r["pairsm"], wm)
-    r["gf"][here] = coarse_low(r["pairsm"], half_t // 2, half_y, 32, r["tmp"])
-    gather_start(r["gf"], sems["low_f"], counts)
 
     planes, rows, lanes = dims = (4 * counts["gx"], 4 * counts["gy"], 32 * counts["gz"])
     pad = wm // 2
@@ -683,7 +706,7 @@
     cell = (cell + 128) // 2 - 64
     wanted = (goal < 64 + wm) | (goal >= 128 - wm)
     matrix = jnp.where((iota((lanes, 128), 0) == 32 * at["gz"] + cell) & wanted, 1.0, 0.0).astype(F32)
-    spread = dot(r["local"][...].reshape(16 * around_low, lanes), matrix).reshape(around_low, 16, 128)
+    spread = pick(r["local"][...].reshape(16 * around_low, lanes), matrix).reshape(around_low, 16, 128)
     for q in range(around_low):
         wide = r["wide"].at[q]
         for k in range(2):
@@ -711,7 +734,7 @@
     for t in range(fine.t):
         red, black = (v0[c][fine.wt + t, 0 : fine.y, :] for c in range(2))
         r["joined"][t] = swap(jnp.where(lane < 64, red, pltpu.roll(black, 64, 1)), t)
-    joined = dot(r["joined"][...].reshape(fine.t * fine.y, 128), split_lanes(True))
+    joined = pick(r["joined"][...].reshape(fine.t * fine.y, 128), split_lanes(True))
     out[...] = joined.reshape(out.shape)
 
 
@@ -743,10 +766,9 @@
         slots=pltpu.VMEM(old_slots.shape, old_slots.dtype), ids=pltpu.VMEM(old_ids.shape, old_ids.dtype),
         owner=pltpu.VMEM(old_owner.shape, old_owner.dtype), coef=vmem(*coefficient.shape), loads=dma(4),
         outgoing=pltpu.VMEM((groups, SEND, cells), BF16), incoming=pltpu.VMEM((groups, SEND, cells), BF16),
-        held=vmem(groups * SEND, cells), sems=dma(9, 2), units=vmem(max(160, devices), 4, 128),
-        lhs=pltpu.VMEM((BOX * BOX, boxes * BOX * BOX), BF16), rhs=pltpu.VMEM((boxes * BOX * BOX, 128), BF16),
-        boxes=vmem(boxes * BOX, 128), pairs=vmem(x // 2, y, 128), pairsm=vmem(x // 4, y // 2, 128),
-        joined=vmem(x, y, 128), tmp=vmem(y // 2, 128), local=vmem(mid.te, 16, lanes),
+        held=vmem(groups * SEND, cells), sems=dma(9, 2), hello=pltpu.SemaphoreType.REGULAR, units=vmem(max(160, devices), 4, 128),
+        rows=vmem(BOX * BOX, 128), pairs=vmem(x // 2, y, 128), pairsm=vmem(x // 4, y // 2, 128),
+        joined=vmem(x, y, 128), tmp=vmem(x * y // 16, 128), local=vmem(mid.te, 16, lanes),
         wide=vmem(max(mid.te, fine.te // 2), 24, 128),
         gk=vmem(counts["gx"], counts["gy"], groups, 4, 128), gf=vmem(counts["gx"], counts["gy"], groups, 4, 128),
         cx=vmem(planes + 1, rows, lanes), v2=vmem(planes, rows, lanes))

time: 28.3 us -> 25.5 us (0.901)
  Pallas kernels: 27.5 us -> 24.7 us
    pallas_call x1, Pallas kernels: 27.5 us -> 24.7 us  [per_device(): pl.pallas_call(functools.partial(kernel, levels, counts, tuple(scratch)),...]
where the time goes in v4:
time: 25.5 us; the launch traced here: 25.3 us
  Pallas kernels  24.7 us (97%)
  local copies, waits for them, and re-layouts  0.66 us (3%)
    pallas_call x1, Pallas kernels, per_device(): pl.pallas_call(functools.partial(kernel, levels, counts, tuple(scratch)),...  24.7 us
    unnamed x1, local copies, waits for them, and re-layouts  0.66 us

profile of v4, /device:TPU:0, one launch (start us, length us, event | category | flops | bytes accessed | tf_op | source)
XLA Modules:
  0.0 25.3 jit_solution(16812108613774623017)
XLA Ops:
  0.0 24.7 %shard_map.46 = f32[16,16,128]{2,1,0:T(8,128)S(1)} custom-call(bf16[1,1,8,4096]{3,2,1,0:T(8,128)(2,1)} %slots_in.1, s32[1,1,8]{2,1,0:T(1,128)} %ids_in.1, s32[1,1,32]{2,1,0:T(1,128)} %owner_in.1, f32[16,16,128]{2,1,0:T(8,128)} %coef_in.1), custom_call_target="tpu_custom_call" | custom-call | tf_op jit(solution)/shard_map/pallas_call | solution.py:779
  24.7 0.7 %copy.6 = f32[16,16,128]{2,1,0:T(8,128)} copy(f32[16,16,128]{2,1,0:T(8,128)S(1)} %shard_map.46) | data formatting | bytes 262144

commit v5 on v4

--- a/solution.py
+++ b/solution.py
@@ -29,7 +29,8 @@
 
 
 class Level:
-    def __init__(self, t, y, wt, wy, h, deep=False):
+    def __init__(self, t, y, wt, wy, h, deep=False, dtype=F32):
+        self.dtype = dtype
         self.t, self.y, self.wt, self.wy, self.h, self.deep = t, y, wt, wy, h, deep
         self.te, self.ye = t + 2 * wt, y + 2 * wy
         self.blocks = y // wy
@@ -41,7 +42,7 @@
         return (self.wt if a else self.t) * (self.wy if b else self.y) // 4 + extra
 
     def scratch(self, tag):
-        vmem = lambda *shape: pltpu.VMEM(shape + (128,), F32)
+        vmem = lambda *shape: pltpu.VMEM(shape + (128,), self.dtype)
         made = {
             "st": vmem(self.t, self.y), "py": vmem(2, self.t, self.wy), "lt": vmem(self.te, self.y),
             "ly": vmem(2, self.te, self.wy), "pf": vmem(self.blocks, self.wy), "pl": vmem(self.blocks, self.wy),
@@ -102,20 +103,20 @@
 
 
 def clear_sides(lv, b):
-    b["lt"][0 : lv.wt] = jnp.zeros((lv.wt, lv.y, 128), F32)
-    b["lt"][lv.t + lv.wt : lv.te] = jnp.zeros((lv.wt, lv.y, 128), F32)
+    b["lt"][0 : lv.wt] = jnp.zeros((lv.wt, lv.y, 128), lv.dtype)
+    b["lt"][lv.t + lv.wt : lv.te] = jnp.zeros((lv.wt, lv.y, 128), lv.dtype)
     for name in ("ly", "lz", "lzb") + (("lk",) if lv.deep else ()):
-        b[name][...] = jnp.zeros(b[name].shape, F32)
+        b[name][...] = jnp.zeros(b[name].shape, lv.dtype)
 
 
 def pack_sides(lv, b):
     h, st, lane = lv.h, b["st"], iota((lv.y, 128), 1)
-    if lv.blocks > 1:
-        b["py"][0] = st[:, 0 : lv.wy, :]
-        b["py"][1] = st[:, lv.y - lv.wy : lv.y, :]
     first = last = jnp.zeros((lv.y, 128), F32)
     for t in range(lv.t):
-        tile = st[t]
+        tile = st[t].astype(F32)
+        if lv.blocks > 1:
+            b["py"][0, t] = tile[0 : lv.wy].astype(lv.dtype)
+            b["py"][1, t] = tile[lv.y - lv.wy : lv.y].astype(lv.dtype)
         for half in range(2):
             at = 2 * h * t + h * half
             turned = pltpu.roll(tile, (at - 64 * half) % 128, 1)
@@ -126,20 +127,24 @@
             b["ky"][1, t : t + 1, :] = tile[lv.y - lv.wy - 1 : lv.y - lv.wy, :]
     for block in range(lv.blocks):
         rows = slice(block * lv.wy, block * lv.wy + lv.wy)
-        b["pf"][block], b["pl"][block] = first[rows], last[rows]
-
-
-def send_sides(lv, b, sems, counts):
+        b["pf"][block], b["pl"][block] = first[rows].astype(lv.dtype), last[rows].astype(lv.dtype)
+
+
+def send_sides(lv, b, sems, counts, axes):
     taken = {-1: (0, lv.wt), 0: (0, lv.t), 1: (lv.t - lv.wt, lv.wt)}
     landed = {-1: lv.t + lv.wt, 0: lv.wt, 1: 0}
-    for x, y, z in reversed(sorted(NEAR, key=lambda n: (n[0] != 0) + (n[1] != 0) + (n[2] != 0))):
-        target, exists = near((x, y, z), counts)
+    pair = counts["gy"] == 2
+    me = lax.axis_index("gy")
+
+    def start(x, y, z):
+        target = near((x, y, z), counts)[0]
         first, count = taken[x]
-        source, goal, side = pl.ds(first, count), pl.ds(landed[x], count), (y + 1) // 2
+        source, goal = pl.ds(first, count), pl.ds(landed[x], count)
+        side = 1 - me if pair else (y + 1) // 2
         if z:
             ends = b["pf"] if z < 0 else b["pl"]
             if y:
-                pairs = [(ends.at[0 if y < 0 else lv.blocks - 1], b["lzb"].at[(1 - z) // 2, 1 - x, (1 - y) // 2])]
+                pairs = [(ends.at[side * (lv.blocks - 1)], b["lzb"].at[(1 - z) // 2, 1 - x, 1 - side])]
             else:
                 pairs = [(ends, b["lz"].at[(1 - z) // 2, 1 - x])]
         elif y:
@@ -149,9 +154,23 @@
         else:
             pairs = [(b["st"].at[source], b["lt"].at[goal])]
         for src, dst in pairs:
-            copy = pltpu.make_async_remote_copy(
-                src, dst, sems.at[0], sems.at[1], device_id=target, device_id_type=MESH)
-            pl.when(exists)(copy.start)
+            pltpu.make_async_remote_copy(
+                src, dst, sems.at[0], sems.at[1], device_id=target, device_id_type=MESH).start()
+
+    steps = (1, 0) if pair else (1, -1, 0)
+    for x, z in sorted(itertools.product((-1, 0, 1), repeat=2), key=lambda n: -abs(n[0]) - abs(n[1])):
+        chosen = [y for y in steps if abs(x) + abs(y) + abs(z) in axes]
+
+        def send():
+            for y in chosen:
+                if pair or not y:
+                    start(x, y, z)
+                else:
+                    pl.when(near((0, y, 0), counts)[1])(functools.partial(start, x, y, z))
+
+        exists = near((x, 0, z), counts)[1]
+        if chosen:
+            send() if exists is None else pl.when(exists)(send)
 
 
 def take_sides(lv, b, sems, counts, units, emit):
@@ -162,7 +181,8 @@
     for a in range(3):
         low, high = [
             jnp.concatenate(
-                [b["lz"][c, a, block] for block in range(lv.blocks)] + [b["lzb"][c, a, 1], b["lzb"][c, a, 0]], axis=0)
+                [b["lz"][c, a, block].astype(F32) for block in range(lv.blocks)]
+                + [b["lzb"][c, a, side].astype(F32) for side in (1, 0)], axis=0)
             for c in range(2)]
         mixed = [jnp.where(((lane - 16 * h * q + h) & 127) < 64, high, low) for q in range(-(-lv.t // 8))]
         place = (0, wt, lv.t + wt)[a]
@@ -170,7 +190,7 @@
         for k in range(count):
             n, t = start + k, place + k
             rows = b["st"][n] if a == 1 else b["lt"][t]
-            full = jnp.concatenate([rows, b["ly"][0, t], b["ly"][1, t]], axis=0)
+            full = jnp.concatenate([part.astype(F32) for part in (rows, b["ly"][0, t], b["ly"][1, t])], axis=0)
             slices = []
             for half in range(2):
                 ends = pltpu.roll(mixed[n // 8], (64 - 2 * h * n - h * half) % 128, 1)
@@ -248,9 +268,9 @@
             if c == 0:
                 zs[x] = same
 
-    batches(0, lv.wt, 2, body)
-    batches(lv.wt, lv.wt + lv.t, 2, functools.partial(body, inside=True))
-    batches(lv.wt + lv.t, lv.te, 2, body)
+    batches(0, lv.wt, 4, body)
+    batches(lv.wt, lv.wt + lv.t, 8, functools.partial(body, inside=True))
+    batches(lv.wt + lv.t, lv.te, 4, body)
 
 
 def around_fine(lv, v, c, x, faces):
@@ -434,7 +454,7 @@
     repeat(planes, body, 0)
 
 
-def bottom(f, s, vv, faces, dims, pad):
+def bottom(f, s, vv, ww, faces, dims, pad):
     planes, rows, lanes = dims
     cx, cy0, cy1, cz0, cz1, cd = faces
 
@@ -449,7 +469,7 @@
 
     def first(p, carry):
         mid, image = operate(f, p)
-        vv[p] = image
+        vv[p + pad] = image
         return carry[0] + mid * mid, carry[1] + mid * image
 
     def total(v):
@@ -458,17 +478,19 @@
     norm, along = repeat(planes, first, (zero, zero))
     alpha = total(norm) / total(along)
 
-    def rest(p, carry):
-        s[p + pad] = f[p + pad] - alpha * vv[p]
+    def second(p, carry):
+        ww[p] = operate(vv, p)[1]
         return carry
 
-    repeat(planes, rest, 0)
-
-    def second(p, carry):
-        mid, image = operate(s, p)
-        return carry[0] + image * mid, carry[1] + image * image
-
-    turned, norm = repeat(planes, second, (zero, zero))
+    repeat(planes, second, 0)
+
+    def last(p, carry):
+        rest = f[p + pad] - alpha * vv[p + pad]
+        image = vv[p + pad] - alpha * ww[p]
+        s[p + pad] = rest
+        return carry[0] + image * rest, carry[1] + image * image
+
+    turned, norm = repeat(planes, last, (zero, zero))
     return alpha, total(turned) / total(norm)
 
 
@@ -538,15 +560,19 @@
         clear_sides(lv, sides[tag])
 
     barrier = pltpu.get_barrier_semaphore()
-    expected = 0
-    for offset in sorted(NEAR, key=lambda n: -sum(map(abs, n))):
-        target, exists = near(offset, counts)
-
-        @pl.when(exists)
-        def _():
-            pl.semaphore_signal(barrier, inc=1, device_id=target, device_id_type=MESH)
-
-        expected = expected + jnp.where(exists, 1, 0)
+    def signal_near(sem, offsets):
+        count = 0
+        for offset in offsets:
+            target, exists = near(offset, counts)
+
+            @pl.when(exists)
+            def _():
+                pl.semaphore_signal(sem, inc=1, device_id=target, device_id_type=MESH)
+
+            count = count + jnp.where(exists, 1, 0)
+        return count
+
+    expected = signal_near(barrier, sorted([n for n in NEAR if 0 in n], key=lambda n: -sum(map(abs, n))))
     others = [{"gz": lax.rem(at["gz"] + k, groups)} for k in range(1, groups)]
     if counts["gx"] > 4 or counts["gy"] > 4:
         for offset in itertools.product(*[range(n) for n in counts.values()]):
@@ -557,11 +583,12 @@
 
     sems = {tag: r["sems"].at[n] for n, tag in enumerate(("k", "c", "f", "g", "q", "e", "move", "low_k", "low_f"))}
 
-    def send(tag):
-        send_sides(levels[tag], sides[tag], sems[tag], counts)
+    def send(tag, axes=(1, 2, 3)):
+        send_sides(levels[tag], sides[tag], sems[tag], counts, axes)
 
     def take(tag, emit):
-        take_sides(levels[tag], sides[tag], sems[tag], counts, units, emit)
+        counted = units if levels[tag].dtype == F32 else r["half_units"]
+        take_sides(levels[tag], sides[tag], sems[tag], counts, counted, emit)
 
     loads[0].wait()
     loads[1].wait()
@@ -575,23 +602,14 @@
         pltpu.make_async_remote_copy(
             r["outgoing"].at[to], r["incoming"].at[me], sems["move"].at[0], sems["move"].at[1],
             device_id={"gz": to}, device_id_type=MESH).start()
-    greeted = 0
-    for offset in itertools.product((-1, 1), (0,), (-1, 0, 1)):
-        target, exists = near(offset, counts)
-
-        @pl.when(exists)
-        def _():
-            pl.semaphore_signal(r["hello"], inc=1, device_id=target, device_id_type=MESH)
-
-        greeted = greeted + jnp.where(exists, 1, 0)
-
+    greeted = signal_near(r["hello"], list(itertools.product((-1, 1), (0,), (-1, 0, 1))))
     loads[2].wait()
     swap = lambda tile, t: jnp.where(even_rows(t, fine.y), tile, pltpu.roll(tile, 64, 1))
     split = pick(coef[...].reshape(fine.t * fine.y, 128), split_lanes(False)).reshape(fine.t, fine.y, 128)
     for t in range(fine.t):
         sides["k"]["st"][t] = swap(split[t], t)
     pack_sides(levels["k"], sides["k"])
-    send("k")
+    send("k", (1, 2))
     r["incoming"][me] = r["outgoing"][me]
 
     half_t, half_y = fine.t // 2, fine.y // 2
@@ -601,6 +619,8 @@
     coarse = 0.125 * fold_rows(r["pairs"], half_y)
     pair_planes([coarse[i] for i in range(half_t)], sides["c"]["st"])
     pack_sides(mid, sides["c"])
+    pl.semaphore_wait(r["hello"], greeted)
+    send("k", (3,))
     send("c")
     for i in range(half_t // 2):
         r["pairsm"][i] = coarse[2 * i] + coarse[2 * i + 1]
@@ -614,9 +634,8 @@
     source = place_boxes(r["incoming"], r["held"], owner, r["rows"], boxes, groups)
     source = source.reshape(fine.t, fine.y, 128)
     for t in range(fine.t):
-        sides["f"]["st"][t] = swap(source[t], t)
+        sides["f"]["st"][t] = swap(source[t], t).astype(BF16)
     pack_sides(fine, sides["f"])
-    pl.semaphore_wait(r["hello"], greeted)
     send("f")
 
     pair_of = lambda name: (r[name + "r"], r[name + "b"])
@@ -655,14 +674,14 @@
     pair_planes([coarse[i] for i in range(half_t)], sides["g"]["st"])
     pack_sides(mid, sides["g"])
     send("g")
+    take("c", store_planes(K1))
+    prepare(K1, *faces1, dd1, iv1)
+    for name in ("k2", "f2", "s2", "v2"):
+        r[name][...] = jnp.zeros(r[name].shape, F32)
     pair_planes([v0[1][fine.wt + x, 0 : fine.y, :] for x in range(fine.t)], sides["q"]["st"])
     pack_sides(levels["q"], sides["q"])
     send("q")
     gather_start(r["gk"], sems["low_k"], counts)
-    take("c", store_planes(K1))
-    prepare(K1, *faces1, dd1, iv1)
-    for name in ("k2", "f2", "s2"):
-        r[name][...] = jnp.zeros(r[name].shape, F32)
     wm = 2 * mid.wt
     parity = iota((mid.ye, 128), 0) + iota((mid.ye, 128), 1)
 
@@ -692,7 +711,7 @@
     take("e", store_planes(E1))
     gather_wait(sems["low_f"], counts, units)
     spread_low(r["gf"], r["f2"], counts, pad)
-    alpha, omega = bottom(r["f2"], r["s2"], r["v2"], low, dims, pad)
+    alpha, omega = bottom(r["f2"], r["s2"], r["v2"], r["w2"], low, dims, pad)
     around_low = mid.te
     for q in range(around_low):
         turned = alpha * r["f2"][4 * at["gx"] + q] + omega * r["s2"][4 * at["gx"] + q]
@@ -745,7 +764,7 @@
     cells = old_slots.shape[3]
     mid = Level(x // 4, y // 2, 3, 8, 6)
     levels = {
-        "k": Level(x, y, 5, 4, 3, deep=True), "f": Level(x, y, 4, 4, 2), "q": Level(x // 2, y, 2, 4, 2),
+        "k": Level(x, y, 5, 4, 3, deep=True), "f": Level(x, y, 4, 4, 2, dtype=BF16), "q": Level(x // 2, y, 2, 4, 2),
         "c": mid, "g": mid, "e": mid}
     fine, edge = levels["f"], levels["k"]
     pad = mid.wt
@@ -767,14 +786,15 @@
         owner=pltpu.VMEM(old_owner.shape, old_owner.dtype), coef=vmem(*coefficient.shape), loads=dma(4),
         outgoing=pltpu.VMEM((groups, SEND, cells), BF16), incoming=pltpu.VMEM((groups, SEND, cells), BF16),
         held=vmem(groups * SEND, cells), sems=dma(9, 2), hello=pltpu.SemaphoreType.REGULAR, units=vmem(max(160, devices), 4, 128),
+        half_units=pltpu.VMEM((160, 4, 128), BF16),
         rows=vmem(BOX * BOX, 128), pairs=vmem(x // 2, y, 128), pairsm=vmem(x // 4, y // 2, 128),
         joined=vmem(x, y, 128), tmp=vmem(x * y // 16, 128), local=vmem(mid.te, 16, lanes),
         wide=vmem(max(mid.te, fine.te // 2), 24, 128),
         gk=vmem(counts["gx"], counts["gy"], groups, 4, 128), gf=vmem(counts["gx"], counts["gy"], groups, 4, 128),
-        cx=vmem(planes + 1, rows, lanes), v2=vmem(planes, rows, lanes))
+        cx=vmem(planes + 1, rows, lanes), w2=vmem(planes, rows, lanes))
     for name in ("cy0", "cy1", "cz0", "cz1", "cd"):
         scratch[name] = vmem(planes, rows, lanes)
-    for name in ("f2", "k2", "s2"):
+    for name in ("f2", "k2", "s2", "v2"):
         scratch[name] = vmem(planes + 2 * pad, rows, lanes)
     return pl.pallas_call(
         functools.partial(kernel, levels, counts, tuple(scratch)),

time: 25.5 us -> 24.7 us (0.969)
  Pallas kernels: 24.7 us -> 23.9 us
    pallas_call x1, Pallas kernels: 24.7 us -> 23.9 us  [per_device(): pl.pallas_call(functools.partial(kernel, levels, counts, tuple(scratch)),...]
where the time goes in v5:
time: 24.7 us; the launch traced here: 24.5 us
  Pallas kernels  23.9 us (97%)
  local copies, waits for them, and re-layouts  0.66 us (3%)
    pallas_call x1, Pallas kernels, per_device(): pl.pallas_call(functools.partial(kernel, levels, counts, tuple(scratch)),...  23.9 us
    unnamed x1, local copies, waits for them, and re-layouts  0.66 us

profile of v5, /device:TPU:0, one launch (start us, length us, event | category | flops | bytes accessed | tf_op | source)
XLA Modules:
  0.0 24.5 jit_solution(15721819083452507661)
XLA Ops:
  0.0 23.9 %shard_map.46 = f32[16,16,128]{2,1,0:T(8,128)S(1)} custom-call(bf16[1,1,8,4096]{3,2,1,0:T(8,128)(2,1)} %slots_in.1, s32[1,1,8]{2,1,0:T(1,128)} %ids_in.1, s32[1,1,32]{2,1,0:T(1,128)} %owner_in.1, f32[16,16,128]{2,1,0:T(8,128)} %coef_in.1), custom_call_target="tpu_custom_call" | custom-call | tf_op jit(solution)/shard_map/pallas_call | solution.py:799
  23.9 0.7 %copy.6 = f32[16,16,128]{2,1,0:T(8,128)} copy(f32[16,16,128]{2,1,0:T(8,128)S(1)} %shard_map.46) | data formatting | bytes 262144

commit v6 on v5

--- a/solution.py
+++ b/solution.py
@@ -309,56 +309,61 @@
     batches(0, lv.t // 2, lv.t // 2, body)
 
 
-def prepare(k, fx, fy, fz, dd, iv):
-    planes = k.shape[0]
-
-    def body(first, count):
-        made = []
-        for x in [first + i for i in range(count)]:
-            kx = k[x]
-            below = 0.5 * (k[jnp.maximum(x - 1, 0)] + kx)
-            above = 0.5 * (kx + k[jnp.minimum(x + 1, planes - 1)])
-            second = 0.5 * (up(kx, 0) + kx)
-            third = 0.5 * (up(kx, 1) + kx)
-            total = below + above + second + down(second, 0) + third + down(third, 1)
-            made.append((x, below, second, third, total, jnp.where(kx > 0.0, 1.0 / total, 0.0)))
-        for x, *values in made:
-            for ref, value in zip((fx, fy, fz, dd, iv), values):
-                ref[x] = value
-
-    batches(0, planes, 4, body)
-
-
-def around(v, x, mid, faces):
-    fx, fy, fz = faces
-    second, third = fy[x], fz[x]
-    summed = fx[x] * v[x - 1] + fx[x + 1] * v[x + 1]
-    summed = summed + second * up(mid, 0) + down(second * mid, 0)
-    return summed + third * up(mid, 1) + down(third * mid, 1)
-
-
-def half_sweep(v, g, faces, iv, colour, low, high):
-    parity = iota(v.shape[1:], 0) + iota(v.shape[1:], 1)
-
-    def body(first, count):
-        fresh = []
-        for x in [first + i for i in range(count)]:
-            mid = v[x]
-            value = (g[x] + around(v, x, mid, faces)) * iv[x]
-            fresh.append((x, jnp.where(((parity + x) & 1) == colour, value, mid)))
-        for x, value in fresh:
-            v[x] = value
-
-    batches(low, high, high - low, body)
-
-
-def residual_pairs(v, g, faces, dd, pairs, halo):
-    for i in range(pairs.shape[0]):
-        total = jnp.zeros(v.shape[1:], F32)
-        for x in (halo + 2 * i, halo + 2 * i + 1):
-            mid = v[x]
-            total = total + (g[x] - dd[x] * mid + around(v, x, mid, faces))
-        pairs[i] = 0.25 * total[0 : pairs.shape[1]]
+def even_cells(shape):
+    return ((iota(shape, 0) + iota(shape, 1)) & 1) == 0
+
+
+def merge_planes(first, second):
+    even = even_cells(first.shape)
+    return jnp.where(even, first, second), jnp.where(even, second, first)
+
+
+def beside(v, c, t):
+    low, high = v[1 - c][max(t - 1, 0)], v[1 - c][min(t + 1, v[1 - c].shape[0] - 1)]
+    even = even_cells(low.shape)
+    return jnp.where(even, low, high) if c == 0 else jnp.where(even, high, low)
+
+
+def prepare_mid(k, xs, xo, fy, fz, dd, iv):
+    for t in range(xs.shape[0]):
+        same = 0.5 * (k[0][t] + k[1][t])
+        xs[t] = same
+        second, third = [], []
+        for c in range(2):
+            second.append(0.5 * (up(k[1 - c][t], 0) + k[c][t]))
+            third.append(0.5 * (up(k[1 - c][t], 1) + k[c][t]))
+        for c in range(2):
+            o, kx = 1 - c, k[c][t]
+            other = 0.5 * (beside(k, c, t) + kx)
+            total = same + other + second[c] + down(second[o], 0) + third[c] + down(third[o], 1)
+            xo[c][t], fy[c][t], fz[c][t], dd[c][t] = other, second[c], third[c], total
+            iv[c][t] = jnp.where(kx > 0.0, 1.0 / total, 0.0)
+
+
+def around_mid(v, c, t, faces):
+    xs, xo, fy, fz = faces
+    o = 1 - c
+    mid = v[o][t]
+    summed = xs[t] * mid + xo[c][t] * beside(v, c, t)
+    summed = summed + fy[c][t] * up(mid, 0) + down(fy[o][t] * mid, 0)
+    return summed + fz[c][t] * up(mid, 1) + down(fz[o][t] * mid, 1)
+
+
+def half_sweep_mid(lv, v, g, faces, iv, c, reach):
+    low, high = 2 * lv.wt - reach, 2 * (lv.wt + lv.t) + reach
+    fresh = [
+        (t, (g[c][t] + around_mid(v, c, t, faces)) * iv[c][t]) for t in range(low // 2, (high + 1) // 2)]
+    for t, value in fresh:
+        v[c][t] = value
+
+
+def residual_mid(lv, v, g, faces, dd, pairs):
+    for i in range(lv.t):
+        t = lv.wt + i
+        total = 0.0
+        for c in range(2):
+            total = total + (g[c][t] - dd[c][t] * v[c][t] + around_mid(v, c, t, faces))
+        pairs[i] = 0.25 * total[0 : lv.y]
 
 
 def pair_planes(planes, target):
@@ -517,7 +522,7 @@
         outgoing[t] = total[SEND * t : SEND * t + SEND, :].astype(BF16)
 
 
-def place_boxes(incoming, held, owner, rows, boxes, groups):
+def choose_boxes(owner, boxes):
     me = lax.axis_index("gz")
     owners = jnp.broadcast_to(owner[0].astype(F32), (boxes, owner.shape[2]))
     here = iota(owners.shape, 1) == iota(owners.shape, 0) + me * boxes
@@ -527,6 +532,10 @@
     row = jnp.sum(jnp.where(first == second, cols, 0.0), axis=0, keepdims=True)
     before = (jnp.broadcast_to(row, (boxes, boxes)) == cols) & (second < first)
     pick = col * SEND + jnp.sum(jnp.where(before, 1.0, 0.0), axis=1, keepdims=True)
+    return pick
+
+
+def place_boxes(incoming, held, pick, rows, boxes, groups):
     for t in range(groups):
         held[SEND * t : SEND * t + SEND, :] = incoming[t].astype(F32)
     per = 128 // BOX
@@ -617,7 +626,8 @@
         pair = sides["k"]["st"][2 * i] + sides["k"]["st"][2 * i + 1]
         r["pairs"][i] = pair + pltpu.roll(pair, 64, 1)
     coarse = 0.125 * fold_rows(r["pairs"], half_y)
-    pair_planes([coarse[i] for i in range(half_t)], sides["c"]["st"])
+    merged = [merge_planes(coarse[i], coarse[i + 1]) for i in range(0, half_t, 2)]
+    pair_planes([plane for pair in merged for plane in pair], sides["c"]["st"])
     pack_sides(mid, sides["c"])
     pl.semaphore_wait(r["hello"], greeted)
     send("k", (3,))
@@ -627,11 +637,12 @@
     here = (at["gx"], at["gy"], at["gz"])
     r["gk"][here] = coarse_low(r["pairsm"], r["tmp"])
     loads[3].wait()
+    r["pick"][...] = jnp.broadcast_to(choose_boxes(owner, boxes), r["pick"].shape)
     if groups > 1:
         part = r["incoming"].at[pl.ds(0, groups - 1)]
         for n in range(2):
             pltpu.make_async_copy(part, part, sems["move"].at[n]).wait()
-    source = place_boxes(r["incoming"], r["held"], owner, r["rows"], boxes, groups)
+    source = place_boxes(r["incoming"], r["held"], r["pick"][...], r["rows"], boxes, groups)
     source = source.reshape(fine.t, fine.y, 128)
     for t in range(fine.t):
         sides["f"]["st"][t] = swap(source[t], t).astype(BF16)
@@ -642,8 +653,8 @@
     v0, g0, k0 = pair_of("v0"), pair_of("g0"), pair_of("k0")
     fx, fy, zo, dd0, iv0 = (pair_of(name) for name in ("fx0", "fy0", "zo0", "dd0", "iv0"))
     faces0 = (fx, fy, r["zs0"], zo)
-    faces1 = (r["fx1"], r["fy1"], r["fz1"])
-    dd1, iv1, v1, K1, G1, E1 = (r[name] for name in ("dd1", "iv1", "v1", "K1", "G1", "E1"))
+    fx1, fy1, fz1, dd1, iv1, v1, g1, k1 = (pair_of(n) for n in ("fx1", "fy1", "fz1", "dd1", "iv1", "v1", "g1", "k1"))
+    faces1 = (r["xs1"], fx1, fy1, fz1)
 
     def store_pair(refs):
         def emit(t, first, second):
@@ -671,11 +682,12 @@
     residual_fine(fine, v0, g0, faces0, dd0, r["pairs"])
 
     coarse = 0.5 * fold_rows(r["pairs"], half_y)
-    pair_planes([coarse[i] for i in range(half_t)], sides["g"]["st"])
+    merged = [merge_planes(coarse[i], coarse[i + 1]) for i in range(0, half_t, 2)]
+    pair_planes([plane for pair in merged for plane in pair], sides["g"]["st"])
     pack_sides(mid, sides["g"])
     send("g")
-    take("c", store_planes(K1))
-    prepare(K1, *faces1, dd1, iv1)
+    take("c", store_pair(k1))
+    prepare_mid(k1, *faces1, dd1, iv1)
     for name in ("k2", "f2", "s2", "v2"):
         r[name][...] = jnp.zeros(r[name].shape, F32)
     pair_planes([v0[1][fine.wt + x, 0 : fine.y, :] for x in range(fine.t)], sides["q"]["st"])
@@ -683,21 +695,19 @@
     send("q")
     gather_start(r["gk"], sems["low_k"], counts)
     wm = 2 * mid.wt
-    parity = iota((mid.ye, 128), 0) + iota((mid.ye, 128), 1)
-
-    def open_mid(t, *planes):
-        for k, plane in enumerate(planes):
-            x = 2 * t + k
-            G1[x] = plane
-            v1[x] = jnp.where(((parity + x) & 1) == 0, plane * iv1[x], 0.0)
+
+    def open_mid(t, red, black):
+        g1[0][t] = red
+        g1[1][t] = black
+        v1[0][t] = red * iv1[0][t]
 
     take("g", open_mid)
     for reach, colour in ((3, 1), (2, 0), (1, 1)):
-        half_sweep(v1, G1, faces1, iv1, colour, wm - reach, wm + half_t + reach)
-    residual_pairs(v1, G1, faces1, dd1, r["pairsm"], wm)
+        half_sweep_mid(mid, v1, g1, faces1, iv1, colour, reach)
+    residual_mid(mid, v1, g1, faces1, dd1, r["pairsm"])
     r["gf"][here] = coarse_low(r["pairsm"], r["tmp"])
     gather_start(r["gf"], sems["low_f"], counts)
-    pair_planes([v1[wm + x, 0 : mid.y, :] for x in range(half_t)], sides["e"]["st"])
+    pair_planes([v1[c][mid.wt + t, 0 : mid.y, :] for t in range(mid.t) for c in range(2)], sides["e"]["st"])
     pack_sides(mid, sides["e"])
     send("e")
 
@@ -708,7 +718,7 @@
     gather_wait(sems["low_k"], counts, units)
     spread_low(r["gk"], r["k2"], counts, pad)
     low_faces(r["k2"], low, dims, pad)
-    take("e", store_planes(E1))
+    take("e", store_pair(v1))
     gather_wait(sems["low_f"], counts, units)
     spread_low(r["gf"], r["f2"], counts, pad)
     alpha, omega = bottom(r["f2"], r["s2"], r["v2"], r["w2"], low, dims, pad)
@@ -730,19 +740,18 @@
         wide = r["wide"].at[q]
         for k in range(2):
             wide[pl.ds(k, 12, stride=2), :] = spread[q, 0:12]
-        for k in range(2):
-            x = 2 * q + k
-            E1[x] = jnp.where(K1[x] > 0.0, E1[x] + wide[...], 0.0)
+        v1[1][q] = jnp.where(k1[1][q] > 0.0, v1[1][q] + wide[...], 0.0)
     for reach, colour in ((5, 0), (4, 1), (3, 0), (2, 1)):
-        half_sweep(E1, G1, faces1, iv1, colour, wm - reach, wm + half_t + reach)
+        half_sweep_mid(mid, v1, g1, faces1, iv1, colour, reach)
 
     low_w = fine.wt // 2
     row = iota((8, 128), 0)
     for i in range(half_t + 2 * low_w):
         x = wm - low_w + i
         wide = r["wide"].at[i]
-        ends = jnp.where(row < low_w, E1[x, 8:16, :], pltpu.roll(E1[x, mid.ye - 8 : mid.ye, :], 4, 0))
-        turned = jnp.concatenate([E1[x, 0:8, :], ends[0:4]], axis=0)
+        plane = merge_planes(v1[0][x // 2], v1[1][x // 2])[x % 2]
+        ends = jnp.where(row < low_w, plane[8:16], pltpu.roll(plane[mid.ye - 8 : mid.ye], 4, 0))
+        turned = jnp.concatenate([plane[0:8], ends[0:4]], axis=0)
         for k in range(2):
             wide[pl.ds(k, 12, stride=2), :] = turned
         for k in range(2):
@@ -779,15 +788,17 @@
             scratch[name + colour] = vmem(edge.te if name == "k0" else fine.te, fine.ye, 128)
     for name in ("zs0", "q0"):
         scratch[name] = vmem(fine.te, fine.ye, 128)
-    for name in ("fx1", "fy1", "fz1", "dd1", "iv1", "v1", "K1", "G1", "E1"):
-        scratch[name] = vmem(2 * mid.te, mid.ye, 128)
+    for name in ("fx1", "fy1", "fz1", "dd1", "iv1", "v1", "g1", "k1"):
+        for colour in "rb":
+            scratch[name + colour] = vmem(mid.te, mid.ye, 128)
+    scratch["xs1"] = vmem(mid.te, mid.ye, 128)
     scratch.update(
         slots=pltpu.VMEM(old_slots.shape, old_slots.dtype), ids=pltpu.VMEM(old_ids.shape, old_ids.dtype),
         owner=pltpu.VMEM(old_owner.shape, old_owner.dtype), coef=vmem(*coefficient.shape), loads=dma(4),
         outgoing=pltpu.VMEM((groups, SEND, cells), BF16), incoming=pltpu.VMEM((groups, SEND, cells), BF16),
         held=vmem(groups * SEND, cells), sems=dma(9, 2), hello=pltpu.SemaphoreType.REGULAR, units=vmem(max(160, devices), 4, 128),
         half_units=pltpu.VMEM((160, 4, 128), BF16),
-        rows=vmem(BOX * BOX, 128), pairs=vmem(x // 2, y, 128), pairsm=vmem(x // 4, y // 2, 128),
+        rows=vmem(BOX * BOX, 128), pick=vmem(boxes, 128), pairs=vmem(x // 2, y, 128), pairsm=vmem(x // 4, y // 2, 128),
         joined=vmem(x, y, 128), tmp=vmem(x * y // 16, 128), local=vmem(mid.te, 16, lanes),
         wide=vmem(max(mid.te, fine.te // 2), 24, 128),
         gk=vmem(counts["gx"], counts["gy"], groups, 4, 128), gf=vmem(counts["gx"], counts["gy"], groups, 4, 128),

time: 24.7 us -> 24.4 us (0.988)
  Pallas kernels: 23.9 us -> 23.6 us
    pallas_call x1, Pallas kernels: 23.9 us -> 23.6 us  [per_device(): pl.pallas_call(functools.partial(kernel, levels, counts, tuple(scratch)),...]
where the time goes in v6:
time: 24.4 us; the launch traced here: 24.3 us
  Pallas kernels  23.6 us (97%)
  local copies, waits for them, and re-layouts  0.66 us (3%)
    pallas_call x1, Pallas kernels, per_device(): pl.pallas_call(functools.partial(kernel, levels, counts, tuple(scratch)),...  23.6 us
    unnamed x1, local copies, waits for them, and re-layouts  0.66 us

profile of v6, /device:TPU:0, one launch (start us, length us, event | category | flops | bytes accessed | tf_op | source)
XLA Modules:
  0.0 24.3 jit_solution(3290145511214874891)
XLA Ops:
  0.0 23.6 %shard_map.46 = f32[16,16,128]{2,1,0:T(8,128)S(1)} custom-call(bf16[1,1,8,4096]{3,2,1,0:T(8,128)(2,1)} %slots_in.1, s32[1,1,8]{2,1,0:T(1,128)} %ids_in.1, s32[1,1,32]{2,1,0:T(1,128)} %owner_in.1, f32[16,16,128]{2,1,0:T(8,128)} %coef_in.1), custom_call_target="tpu_custom_call" | custom-call | tf_op jit(solution)/shard_map/pallas_call | solution.py:810
  23.6 0.7 %copy.6 = f32[16,16,128]{2,1,0:T(8,128)} copy(f32[16,16,128]{2,1,0:T(8,128)S(1)} %shard_map.46) | data formatting | bytes 262144

commit v7 on v6

--- a/solution.py
+++ b/solution.py
@@ -155,7 +155,7 @@
             pairs = [(b["st"].at[source], b["lt"].at[goal])]
         for src, dst in pairs:
             pltpu.make_async_remote_copy(
-                src, dst, sems.at[0], sems.at[1], device_id=target, device_id_type=MESH).start()
+                src, dst, sems[0], sems[1], device_id=target, device_id_type=MESH).start()
 
     steps = (1, 0) if pair else (1, -1, 0)
     for x, z in sorted(itertools.product((-1, 0, 1), repeat=2), key=lambda n: -abs(n[0]) - abs(n[1])):
@@ -175,7 +175,7 @@
 
 def take_sides(lv, b, sems, counts, units, emit):
     h, wt = lv.h, lv.wt
-    wait_near(lv, counts, units, (sems.at[0], sems.at[1]))
+    wait_near(lv, counts, units, sems)
     lane = iota((lv.ye, 128), 1)
     own, edge = lane < 64, (lane < 64 + h) | (lane >= 128 - h)
     for a in range(3):
@@ -209,14 +209,14 @@
                 axis: lax.rem(me[axis] + jnp.where(me[axis] < counts[axis] // 2, k, counts[axis] - k), counts[axis])
                 for axis, k in zip(counts, offset) if k}
             pltpu.make_async_remote_copy(
-                mine, mine, sems.at[0], sems.at[1], device_id=target, device_id_type=MESH).start()
+                mine, mine, sems[0], sems[1], device_id=target, device_id_type=MESH).start()
 
 
 def gather_wait(sems, counts, units):
     others = counts["gx"] * counts["gy"] * counts["gz"] - 1
     if others:
-        wait_units(units, others, sems.at[0])
-        wait_units(units, others, sems.at[1])
+        wait_units(units, others, sems[0])
+        wait_units(units, others, sems[1])
 
 
 def batches(low, high, size, body):
@@ -394,6 +394,11 @@
     return jnp.where(lane == cell // 2 + 64 * (cell % 2), 1.0, 0.0).astype(F32)
 
 
+def split_both(transposed):
+    matrix = split_lanes(transposed)
+    return jnp.concatenate([matrix, pltpu.roll(matrix, 64, 1 - int(transposed))], axis=1)
+
+
 def coarse_low(pairs, tmp):
     count, rows, _ = pairs.shape
     half = rows // 2
@@ -499,7 +504,7 @@
     return alpha, total(turned) / total(norm)
 
 
-def pack_boxes(slots, ids, outgoing, boxes, groups):
+def choose_slots(ids, boxes, groups):
     held = ids[0].astype(F32)
     cap = held.shape[1]
     eye = iota((cap, cap), 0) == iota((cap, cap), 1)
@@ -514,11 +519,16 @@
     send_row = jnp.where(held >= 0.0, target(held) * SEND + ranking, -1.0)
     count = groups * SEND
     picker = jnp.where(iota((count, cap), 0).astype(F32) == jnp.broadcast_to(send_row, (count, cap)), 1.0, 0.0)
+    return picker
+
+
+def pack_boxes(slots, picker, outgoing):
+    count, cap = picker.shape
     data = slots[0, 0].astype(F32)
     total = jnp.zeros((count, data.shape[1]), F32)
     for q in range(cap):
         total = total + picker[:, q : q + 1] * data[q : q + 1, :]
-    for t in range(groups):
+    for t in range(outgoing.shape[0]):
         outgoing[t] = total[SEND * t : SEND * t + SEND, :].astype(BF16)
 
 
@@ -550,7 +560,7 @@
             moved = pltpu.roll(pltpu.roll(chosen, BOX * d, 1), boxes - d, 0)
             total = jnp.where(((lane_box - row) & (boxes - 1)) == d, moved, total)
         rows[per * part : per * part + per, :] = total
-    return jnp.dot(rows[...].astype(BF16), split_lanes(False).astype(BF16), preferred_element_type=F32)
+    return jnp.dot(rows[...].astype(BF16), split_both(False).astype(BF16), preferred_element_type=F32)
 
 
 def kernel(levels, counts, names, slots_in, ids_in, owner_in, coef_in, out, *scratch):
@@ -558,9 +568,12 @@
     groups = counts["gz"]
     at = {axis: lax.axis_index(axis) for axis in counts}
     slots, ids, owner, coef, units = r["slots"], r["ids"], r["owner"], r["coef"], r["units"]
+    turns = (("move", "g", "low_f"), ("k", "q"), ("f", "low_k"), ("c", "e"))
+    sends = {tag: n for n, tags in enumerate(turns) for tag in tags}
+    sems = {tag: (r["sems"].at[n], r["sems"].at[len(turns) + k]) for k, (tag, n) in enumerate(sends.items())}
     loads = [
-        pltpu.make_async_copy(source, target, r["loads"].at[n])
-        for n, (source, target) in enumerate(((slots_in, slots), (ids_in, ids), (coef_in, coef), (owner_in, owner)))]
+        pltpu.make_async_copy(source, target, r["sems"].at[n])
+        for n, (source, target) in enumerate(((ids_in, ids), (slots_in, slots), (coef_in, coef), (owner_in, owner)))]
     for load in loads:
         load.start()
     fine, mid = levels["f"], levels["g"]
@@ -590,8 +603,6 @@
     for target in others:
         pl.semaphore_signal(barrier, inc=1, device_id=target, device_id_type=MESH)
 
-    sems = {tag: r["sems"].at[n] for n, tag in enumerate(("k", "c", "f", "g", "q", "e", "move", "low_k", "low_f"))}
-
     def send(tag, axes=(1, 2, 3)):
         send_sides(levels[tag], sides[tag], sems[tag], counts, axes)
 
@@ -600,23 +611,25 @@
         take_sides(levels[tag], sides[tag], sems[tag], counts, counted, emit)
 
     loads[0].wait()
+    boxes = out.shape[2] // BOX
+    picker = choose_slots(ids, boxes, groups)
     loads[1].wait()
-    boxes = out.shape[2] // BOX
-    pack_boxes(slots, ids, r["outgoing"], boxes, groups)
+    pack_boxes(slots, picker, r["outgoing"])
     pl.semaphore_wait(barrier, expected + len(others))
 
     me = at["gz"]
     for k in range(1, groups):
         to = lax.rem(me + k, groups)
         pltpu.make_async_remote_copy(
-            r["outgoing"].at[to], r["incoming"].at[me], sems["move"].at[0], sems["move"].at[1],
+            r["outgoing"].at[to], r["incoming"].at[me], sems["move"][0], sems["move"][1],
             device_id={"gz": to}, device_id_type=MESH).start()
     greeted = signal_near(r["hello"], list(itertools.product((-1, 1), (0,), (-1, 0, 1))))
     loads[2].wait()
-    swap = lambda tile, t: jnp.where(even_rows(t, fine.y), tile, pltpu.roll(tile, 64, 1))
-    split = pick(coef[...].reshape(fine.t * fine.y, 128), split_lanes(False)).reshape(fine.t, fine.y, 128)
+    loads[3].wait()
+    choose = lambda both, t: jnp.where(even_rows(t, fine.y), both[t, :, 0:128], both[t, :, 128:256])
+    split = pick(coef[...].reshape(fine.t * fine.y, 128), split_both(False)).reshape(fine.t, fine.y, 256)
     for t in range(fine.t):
-        sides["k"]["st"][t] = swap(split[t], t)
+        sides["k"]["st"][t] = choose(split, t)
     pack_sides(levels["k"], sides["k"])
     send("k", (1, 2))
     r["incoming"][me] = r["outgoing"][me]
@@ -636,16 +649,15 @@
         r["pairsm"][i] = coarse[2 * i] + coarse[2 * i + 1]
     here = (at["gx"], at["gy"], at["gz"])
     r["gk"][here] = coarse_low(r["pairsm"], r["tmp"])
-    loads[3].wait()
     r["pick"][...] = jnp.broadcast_to(choose_boxes(owner, boxes), r["pick"].shape)
     if groups > 1:
         part = r["incoming"].at[pl.ds(0, groups - 1)]
         for n in range(2):
-            pltpu.make_async_copy(part, part, sems["move"].at[n]).wait()
+            pltpu.make_async_copy(part, part, sems["move"][n]).wait()
     source = place_boxes(r["incoming"], r["held"], r["pick"][...], r["rows"], boxes, groups)
-    source = source.reshape(fine.t, fine.y, 128)
+    source = source.reshape(fine.t, fine.y, 256)
     for t in range(fine.t):
-        sides["f"]["st"][t] = swap(source[t], t).astype(BF16)
+        sides["f"]["st"][t] = choose(source, t).astype(BF16)
     pack_sides(fine, sides["f"])
     send("f")
 
@@ -707,8 +719,8 @@
     residual_mid(mid, v1, g1, faces1, dd1, r["pairsm"])
     r["gf"][here] = coarse_low(r["pairsm"], r["tmp"])
     gather_start(r["gf"], sems["low_f"], counts)
-    pair_planes([v1[c][mid.wt + t, 0 : mid.y, :] for t in range(mid.t) for c in range(2)], sides["e"]["st"])
-    pack_sides(mid, sides["e"])
+    pair_planes([v1[1][mid.wt + t, 0 : mid.y, :] for t in range(mid.t)], sides["e"]["st"])
+    pack_sides(levels["e"], sides["e"])
     send("e")
 
     planes, rows, lanes = dims = (4 * counts["gx"], 4 * counts["gy"], 32 * counts["gz"])
@@ -718,7 +730,14 @@
     gather_wait(sems["low_k"], counts, units)
     spread_low(r["gk"], r["k2"], counts, pad)
     low_faces(r["k2"], low, dims, pad)
-    take("e", store_pair(v1))
+
+    def store_black(t, *planes):
+        for k, plane in enumerate(planes):
+            n = 2 * t + k - (2 * levels["e"].wt - mid.wt)
+            if 0 <= n < mid.te:
+                v1[1][n] = plane
+
+    take("e", store_black)
     gather_wait(sems["low_f"], counts, units)
     spread_low(r["gf"], r["f2"], counts, pad)
     alpha, omega = bottom(r["f2"], r["s2"], r["v2"], r["w2"], low, dims, pad)
@@ -761,9 +780,10 @@
     lane = iota((fine.y, 128), 1)
     for t in range(fine.t):
         red, black = (v0[c][fine.wt + t, 0 : fine.y, :] for c in range(2))
-        r["joined"][t] = swap(jnp.where(lane < 64, red, pltpu.roll(black, 64, 1)), t)
-    joined = pick(r["joined"][...].reshape(fine.t * fine.y, 128), split_lanes(True))
-    out[...] = joined.reshape(out.shape)
+        r["joined"][t] = jnp.where(lane < 64, red, pltpu.roll(black, 64, 1))
+    joined = pick(r["joined"][...].reshape(fine.t * fine.y, 128), split_both(True)).reshape(fine.t, fine.y, 256)
+    for t in range(fine.t):
+        out[t] = choose(joined, t)
 
 
 def per_device(counts, old_slots, old_ids, old_owner, coefficient):
@@ -774,7 +794,7 @@
     mid = Level(x // 4, y // 2, 3, 8, 6)
     levels = {
         "k": Level(x, y, 5, 4, 3, deep=True), "f": Level(x, y, 4, 4, 2, dtype=BF16), "q": Level(x // 2, y, 2, 4, 2),
-        "c": mid, "g": mid, "e": mid}
+        "c": mid, "g": mid, "e": Level(x // 8, y // 2, 2, 8, 6)}
     fine, edge = levels["f"], levels["k"]
     pad = mid.wt
     devices = counts["gx"] * counts["gy"] * groups
@@ -794,9 +814,9 @@
     scratch["xs1"] = vmem(mid.te, mid.ye, 128)
     scratch.update(
         slots=pltpu.VMEM(old_slots.shape, old_slots.dtype), ids=pltpu.VMEM(old_ids.shape, old_ids.dtype),
-        owner=pltpu.VMEM(old_owner.shape, old_owner.dtype), coef=vmem(*coefficient.shape), loads=dma(4),
+        owner=pltpu.VMEM(old_owner.shape, old_owner.dtype), coef=vmem(*coefficient.shape),
         outgoing=pltpu.VMEM((groups, SEND, cells), BF16), incoming=pltpu.VMEM((groups, SEND, cells), BF16),
-        held=vmem(groups * SEND, cells), sems=dma(9, 2), hello=pltpu.SemaphoreType.REGULAR, units=vmem(max(160, devices), 4, 128),
+        held=vmem(groups * SEND, cells), sems=dma(13), hello=pltpu.SemaphoreType.REGULAR, units=vmem(max(160, devices), 4, 128),
         half_units=pltpu.VMEM((160, 4, 128), BF16),
         rows=vmem(BOX * BOX, 128), pick=vmem(boxes, 128), pairs=vmem(x // 2, y, 128), pairsm=vmem(x // 4, y // 2, 128),
         joined=vmem(x, y, 128), tmp=vmem(x * y // 16, 128), local=vmem(mid.te, 16, lanes),

time: 24.4 us -> 24.1 us (0.988)
  Pallas kernels: 23.6 us -> 23.2 us
    pallas_call x1, Pallas kernels: 23.6 us -> 23.2 us  [per_device(): pl.pallas_call(functools.partial(kernel, levels, counts, tuple(scratch)),...]
where the time goes in v7:
time: 24.1 us; the launch traced here: 23.9 us
  Pallas kernels  23.2 us (96%)
  local copies, waits for them, and re-layouts  0.66 us (3%)
    pallas_call x1, Pallas kernels, per_device(): pl.pallas_call(functools.partial(kernel, levels, counts, tuple(scratch)),...  23.2 us
    unnamed x1, local copies, waits for them, and re-layouts  0.66 us

profile of v7, /device:TPU:0, one launch (start us, length us, event | category | flops | bytes accessed | tf_op | source)
XLA Modules:
  0.0 23.9 jit_solution(10112525705447994142)
XLA Ops:
  0.0 23.2 %shard_map.46 = f32[16,16,128]{2,1,0:T(8,128)S(1)} custom-call(bf16[1,1,8,4096]{3,2,1,0:T(8,128)(2,1)} %slots_in.1, s32[1,1,8]{2,1,0:T(1,128)} %ids_in.1, s32[1,1,32]{2,1,0:T(1,128)} %owner_in.1, f32[16,16,128]{2,1,0:T(8,128)} %coef_in.1), custom_call_target="tpu_custom_call" | custom-call | tf_op jit(solution)/shard_map/pallas_call | solution.py:830
  23.2 0.7 %copy.6 = f32[16,16,128]{2,1,0:T(8,128)} copy(f32[16,16,128]{2,1,0:T(8,128)S(1)} %shard_map.46) | data formatting | bytes 262144

commit v8 on v7

--- a/solution.py
+++ b/solution.py
@@ -404,12 +404,13 @@
     half = rows // 2
     for x in range(count):
         tmp[half * x : half * x + half, :] = pairs[x, pl.ds(0, half, stride=2), :] + pairs[x, pl.ds(1, half, stride=2), :]
-    source, goal = iota((128, 128), 0), iota((128, 128), 1)
-    means = 0.125 * pick(tmp[...], jnp.where((source // 2 == goal) & (source < 64), 1.0, 0.0))
-    total = means[0:half]
+    shape = (128, 128 * count)
+    source, goal, x = iota(shape, 0), iota(shape, 1) % 128, iota(shape, 1) // 128
+    means = pick(tmp[...], jnp.where((source // 2 + 32 * x == goal) & (source < 64), 1.0, 0.0))
+    total = means[0:half, 0:128]
     for x in range(1, count):
-        total = total + pltpu.roll(means[half * x : half * x + half], 32 * x, 1)
-    return total
+        total = total + means[half * x : half * x + half, 128 * x : 128 * x + 128]
+    return 0.125 * total
 
 
 def repeat(count, body, carry):

time: 24.1 us -> 24 us (level)
  no operation moved by 1% of the time
where the time goes in v8:
time: 24 us; the launch traced here: 23.8 us
  Pallas kernels  23.2 us (97%)
  local copies, waits for them, and re-layouts  0.66 us (3%)
    pallas_call x1, Pallas kernels, per_device(): pl.pallas_call(functools.partial(kernel, levels, counts, tuple(scratch)),...  23.2 us
    unnamed x1, local copies, waits for them, and re-layouts  0.66 us

profile of v8, /device:TPU:0, one launch (start us, length us, event | category | flops | bytes accessed | tf_op | source)
XLA Modules:
  0.0 23.8 jit_solution(8609293013869373604)
XLA Ops:
  0.0 23.2 %shard_map.46 = f32[16,16,128]{2,1,0:T(8,128)S(1)} custom-call(bf16[1,1,8,4096]{3,2,1,0:T(8,128)(2,1)} %slots_in.1, s32[1,1,8]{2,1,0:T(1,128)} %ids_in.1, s32[1,1,32]{2,1,0:T(1,128)} %owner_in.1, f32[16,16,128]{2,1,0:T(8,128)} %coef_in.1), custom_call_target="tpu_custom_call" | custom-call | tf_op jit(solution)/shard_map/pallas_call | solution.py:831
  23.2 0.7 %copy.6 = f32[16,16,128]{2,1,0:T(8,128)} copy(f32[16,16,128]{2,1,0:T(8,128)S(1)} %shard_map.46) | data formatting | bytes 262144
